TPU v7x, 32 devices: a 4x2x2 block of a 4x4x8 slice. The times are simulated.
32 devices in a mesh: batch: 4 (over y, z), seq: 8 (over x, core).
Axes of the slice: x: 4, y: 2, z: 2, core: 2. Of those that a mesh axis runs over, the one named last changes fastest.
The devices are a block of a 4x4x8 slice.
Arguments:
- msa_act: bfloat16 [4096, 256, 64], P(('batch', 'seq')), parts along dimension 0
- msa_mask: int32 [4096, 256], P(('batch', 'seq')), parts along dimension 0
- pair_act: bfloat16 [1024, 256, 128], P(('batch', 'seq')), parts along dimension 0
- w_pair_bias: bfloat16 [128, 8], replicated
- w_row_in: bfloat16 [64, 256], replicated
- w_row_out: bfloat16 [64, 64], replicated
- w_col_in: bfloat16 [64, 144], replicated
- w_col_out: bfloat16 [64, 64], replicated
- w_trans_in: bfloat16 [64, 256], replicated
- w_trans_out: bfloat16 [256, 64], replicated
Outputs:
- output: bfloat16 [4096, 256, 64], P('batch', 'seq'), parts along dimension 0
There are 4 independent parts. A program takes and returns all parts, laid end to end along the dimension named above; an argument that names none is the same for every part.
All inputs are finite; a program needn't handle non-finite values.
Results may differ from a plain program's by a relative error of at most 0.013669.
Values are sent between devices in bfloat16 or wider.
A program may use at most 768 MiB of HBM per device.

v0:
```python
import jax
import jax.numpy as jnp
from jax import lax
from jax.sharding import PartitionSpec as P

LN_EPS = 1.0e-5
MASK_BIG = 1.0e9
MEAN_EPS = 1.0e-10


def layer_norm(x_in):
    x_f32 = x_in.astype(jnp.float32)
    mean_val = jnp.mean(x_f32, axis=-1, keepdims=True)
    centered = x_f32 - mean_val
    var_val = jnp.mean(centered * centered, axis=-1, keepdims=True)
    return (centered * lax.rsqrt(var_val + LN_EPS)).astype(jnp.bfloat16)


def pick_tile(n_rows, per_row):
    budget = 2 ** 22
    best_tile = 1
    for candidate in range(1, n_rows + 1):
        if n_rows % candidate == 0 and candidate * per_row <= budget:
            best_tile = candidate
    return best_tile


def row_attention(value_a7, mask_bias, bias_hij, w_row_in, w_row_out):
    n_seq, n_res, n_chans = value_a7.shape
    n_heads = bias_hij.shape[0]
    head_dim = w_row_out.shape[0] // n_heads
    qk_scale = head_dim ** -0.5
    w_row_split = w_row_in.reshape(n_chans, 4, n_heads, head_dim)
    row_proj = jnp.einsum('snc,cfhd->fsnhd', layer_norm(value_a7), w_row_split, preferred_element_type=jnp.float32).astype(jnp.bfloat16)
    tile_rows = pick_tile(n_seq, n_heads * n_res * n_res)
    n_tiles = n_seq // tile_rows
    tiled_proj = row_proj.reshape(4, n_tiles, tile_rows, n_res, n_heads, head_dim)

    def tile_body(packed):
        q_tile, k_tile, v_tile, m_tile = packed
        logits = jnp.einsum('sihd,sjhd->shij', q_tile, k_tile, preferred_element_type=jnp.float32) * qk_scale
        logits = logits + bias_hij[None] + m_tile[:, None, None, :]
        attn_probs = jax.nn.softmax(logits, axis=-1).astype(jnp.bfloat16)
        return jnp.einsum('shij,sjhd->sihd', attn_probs, v_tile, preferred_element_type=jnp.float32)

    attended = lax.map(tile_body, (tiled_proj[0], tiled_proj[1], tiled_proj[2], mask_bias.reshape(n_tiles, tile_rows, n_res)))
    attended = attended.reshape(n_seq, n_res, n_heads, head_dim)
    gated_row = (jax.nn.sigmoid(row_proj[3].astype(jnp.float32)) * attended).astype(jnp.bfloat16)
    row_update = jnp.einsum('snhd,hdc->snc', gated_row, w_row_out.reshape(n_heads, head_dim, n_chans), preferred_element_type=jnp.float32)
    return (value_a7.astype(jnp.float32) + row_update).astype(jnp.bfloat16)


def column_attention(value_a7, value_a8, w_col_in, w_col_out, n_heads):
    n_seq, n_res, n_chans = value_a7.shape
    head_ch = w_col_out.shape[0]
    head_dim = head_ch // n_heads
    col_proj = jnp.einsum('snc,cf->snf', layer_norm(value_a7), w_col_in, preferred_element_type=jnp.float32).astype(jnp.bfloat16)
    queries = col_proj[:, :, :head_ch].reshape(n_seq, n_res, n_heads, head_dim)
    col_keys = col_proj[:, :, head_ch:head_ch + head_dim]
    col_vals = col_proj[:, :, head_ch + head_dim:head_ch + 2 * head_dim]
    col_gates = col_proj[:, :, head_ch + 2 * head_dim:].reshape(n_seq, n_res, n_heads, head_dim)
    mask_f32 = value_a8.astype(jnp.float32)
    q_sum = jnp.einsum('sn,snhd->nhd', value_a8.astype(jnp.bfloat16), queries, preferred_element_type=jnp.float32)
    mask_count = jnp.sum(mask_f32, axis=0)
    q_sum, mask_count = lax.psum((q_sum, mask_count), 'seq')
    q_mean = (q_sum / (mask_count + MEAN_EPS)[:, None, None]).astype(jnp.bfloat16)
    col_logits = jnp.einsum('nhd,snd->snh', q_mean, col_keys, preferred_element_type=jnp.float32) * head_dim ** -0.5
    col_logits = col_logits + (MASK_BIG * (mask_f32 - 1.0))[:, :, None]
    loc_max = jnp.max(col_logits, axis=0)
    weights = jnp.exp(col_logits - loc_max[None])
    loc_den = jnp.sum(weights, axis=0)
    loc_num = jnp.einsum('snh,snd->nhd', weights, col_vals, preferred_element_type=jnp.float32)
    glob_max = lax.pmax(loc_max, 'seq')
    rescale = jnp.exp(loc_max - glob_max)
    glob_den, glob_num = lax.psum((loc_den * rescale, loc_num * rescale[:, :, None]), 'seq')
    col_out = glob_num / glob_den[:, :, None]
    gated_col = (jax.nn.sigmoid(col_gates.astype(jnp.float32)) * col_out[None]).astype(jnp.bfloat16)
    col_update = jnp.einsum('snhd,hdc->snc', gated_col, w_col_out.reshape(n_heads, head_dim, n_chans), preferred_element_type=jnp.float32)
    return (value_a7.astype(jnp.float32) + col_update).astype(jnp.bfloat16)


def transition(value_a7, w_trans_in, w_trans_out):
    hidden = jnp.einsum('snc,cf->snf', layer_norm(value_a7), w_trans_in, preferred_element_type=jnp.float32)
    hidden = jnp.maximum(hidden, 0.0).astype(jnp.bfloat16)
    trans_update = jnp.einsum('snf,fc->snc', hidden, w_trans_out, preferred_element_type=jnp.float32)
    return (value_a7.astype(jnp.float32) + trans_update).astype(jnp.bfloat16)


def solution(mesh):
    def local_block(value_a7, value_a8, pair_act, w_pair_bias, w_row_in, w_row_out, w_col_in, w_col_out, w_trans_in, w_trans_out):
        n_heads = w_pair_bias.shape[1]
        bias_rows = jnp.einsum('ijc,ch->hij', layer_norm(pair_act), w_pair_bias, preferred_element_type=jnp.float32).astype(jnp.bfloat16)
        bias_full = lax.all_gather(bias_rows, 'seq', axis=1, tiled=True)
        mask_bias = MASK_BIG * (value_a8.astype(jnp.float32) - 1.0)
        after_row = row_attention(value_a7, mask_bias, bias_full, w_row_in, w_row_out)
        after_col = column_attention(after_row, value_a8, w_col_in, w_col_out, n_heads)
        after_trans = transition(after_col, w_trans_in, w_trans_out)
        return lax.all_to_all(after_trans, 'seq', 1, 0, tiled=True)

    rows_spec = P(('batch', 'seq'))
    return jax.shard_map(local_block, mesh=mesh, in_specs=(rows_spec, rows_spec, rows_spec, P(), P(), P(), P(), P(), P(), P()), out_specs=P('batch', 'seq'), check_vma=False)
```

profile of v0, /device:TPU:81, one launch (start us, length us, event | category | flops | bytes accessed | tf_op | source)
XLA Modules:
  0.0 590.4 jit_solution(2693855623977489367)
XLA Ops:
  12.4 4.4 fusion.99
  21.2 4.0 fusion.59
  26.1 14.3 %psum.29 = f32[256]{0:T(256)S(1)} all-reduce(f32[256]{0:T(256)S(1)} %get-tuple-element.99), channel_id=1, replica_groups=mesh['batch'=4,'seq'=8] {'seq'}, use_global_device_ids=true, to_apply=%region_12.13 | all-reduce | flops 256 | bytes 2048 | tf_op jit(solution)/shard_map/psum | solution.py:65
  41.0 10.3 %convert_bitcast_fusion = bf16[4,128,256,8,8]{2,4,3,0,1:T(8,128)(2,1)} fusion(bf16[64,4,8,8,1]{0,3,2,1,4:T(8,128)(2,1)S(1)} %bitcast.135, bf16[128,256,64]{1,2,0:T(8,128)(2,1)} %param.12, f32[128,256]{1,0:T(8,128)S(1)} %add_rsqrt_fusion.2, f32[128,256]{1,0:T(8,128)S(1)} %broadcast_multiply_fusion.2), kind=kOutput, calls=%fused_computation.33 | convolution fusion | flops 1090519040 | bytes 21266432 | tf_op jit(solution)/shard_map/snc,cfhd->fsnhd/dot_general | solution.py:34
  51.3 9.0 %fusion.121 = (bf16[1,128,256,8,8]{2,4,3,0,1:T(8,128)(2,1)}, bf16[1,128,256,8,8]{2,4,3,0,1:T(8,128)(2,1)}, bf16[1,128,256,8,8]{2,4,3,0,1:T(8,128)(2,1)}) fusion(bf16[4,128,256,8,8]{2,4,3,0,1:T(8,128)(2,1)} %convert_bitcast_fusion), kind=kLoop, calls=%fused_computation.122 | loop fusion | bytes 25165824 | tf_op jit(solution)/shard_map/slice | solution.py:46
  61.9 261.3 %while.10 = (s32[]{:T(128)}, f32[16,8,256,8,8]{2,4,3,1,0:T(8,128)}, bf16[16,8,256,8,8]{2,4,3,1,0:T(8,128)(2,1)}, bf16[16,8,256,8,8]{2,4,3,1,0:T(8,128)(2,1)}, bf...) while((s32[]{:T(128)}, f32[16,8,256,8,8]{2,4,3,1,0:T(8,128)}, ...), condition=%wide.region_7.8_spmd, body=%wide.region_4.7_spmd.sunk | while | flops 248005120 | bytes 9342041 | solution.py:46
  62.6 7.1 %fusion.140 = f32[8,8,256]{2,1,0:T(8,128)S(1)} fusion(f32[8,256]{1,0:T(8,128)S(1)} %dynamic-slice_bitcast_fusion.2, f32[8,256,256]{1,2,0:T(8,128)S(1)} %convert_element_type.231, bf16[16,8,256,8,8]{2,4,3,1,0:T(8,128)(2,1)} %get-tuple-element.171, s32[]{:T(128)} %get-tuple-element.159, bf16[16,8,256,8,8]{2,4,3,1,0:T(8,128)(2,1)} %get-tuple-element.170), kind=kOutput, calls=%fused_computation.121.clone.1 | convolution fusion | flops 88080640 | bytes 2696192 | tf_op jit(solution)/shard_map/while/body/eval_jaxpr/sub | solution.py:43
  69.7 8.9 %fusion.141 = f32[16,8,256,8,8]{2,4,3,1,0:T(8,128)} fusion(f32[16,8,256,8,8]{2,4,3,1,0:T(8,128)} %get-tuple-element.160, s32[]{:T(128)} %get-tuple-element.159, f32[8,8,256]{2,1,0:T(8,128)S(1)} %fusion.140, bf16[16,8,256,8,8]{2,4,3,1,0:T(8,128)(2,1)} %get-tuple-element.169, f32[8,256]{1,0:T(8,128)S(1)} %dynamic-slice_bitcast_fusion.2, ...), kind=kOutput, calls=%fused_computation.11.clone.1 | convolution fusion | flops 159400192 | bytes 3483648 | tf_op jit(solution)/shard_map/while/body/eval_jaxpr/shij,sjhd->sihd/dot_general | solution.py:44
  78.9 7.1 %fusion.140 = f32[8,8,256]{2,1,0:T(8,128)S(1)} fusion(f32[8,256]{1,0:T(8,128)S(1)} %dynamic-slice_bitcast_fusion.2, f32[8,256,256]{1,2,0:T(8,128)S(1)} %convert_element_type.231, bf16[16,8,256,8,8]{2,4,3,1,0:T(8,128)(2,1)} %get-tuple-element.171, s32[]{:T(128)} %get-tuple-element.159, bf16[16,8,256,8,8]{2,4,3,1,0:T(8,128)(2,1)} %get-tuple-element.170), kind=kOutput, calls=%fused_computation.121.clone.1 | convolution fusion | flops 88080640 | bytes 2696192 | tf_op jit(solution)/shard_map/while/body/eval_jaxpr/sub | solution.py:43
  86.0 9.0 %fusion.141 = f32[16,8,256,8,8]{2,4,3,1,0:T(8,128)} fusion(f32[16,8,256,8,8]{2,4,3,1,0:T(8,128)} %get-tuple-element.160, s32[]{:T(128)} %get-tuple-element.159, f32[8,8,256]{2,1,0:T(8,128)S(1)} %fusion.140, bf16[16,8,256,8,8]{2,4,3,1,0:T(8,128)(2,1)} %get-tuple-element.169, f32[8,256]{1,0:T(8,128)S(1)} %dynamic-slice_bitcast_fusion.2, ...), kind=kOutput, calls=%fused_computation.11.clone.1 | convolution fusion | flops 159400192 | bytes 3483648 | tf_op jit(solution)/shard_map/while/body/eval_jaxpr/shij,sjhd->sihd/dot_general | solution.py:44
  95.2 7.1 %fusion.140 = f32[8,8,256]{2,1,0:T(8,128)S(1)} fusion(f32[8,256]{1,0:T(8,128)S(1)} %dynamic-slice_bitcast_fusion.2, f32[8,256,256]{1,2,0:T(8,128)S(1)} %convert_element_type.231, bf16[16,8,256,8,8]{2,4,3,1,0:T(8,128)(2,1)} %get-tuple-element.171, s32[]{:T(128)} %get-tuple-element.159, bf16[16,8,256,8,8]{2,4,3,1,0:T(8,128)(2,1)} %get-tuple-element.170), kind=kOutput, calls=%fused_computation.121.clone.1 | convolution fusion | flops 88080640 | bytes 2696192 | tf_op jit(solution)/shard_map/while/body/eval_jaxpr/sub | solution.py:43
  102.3 9.0 %fusion.141 = f32[16,8,256,8,8]{2,4,3,1,0:T(8,128)} fusion(f32[16,8,256,8,8]{2,4,3,1,0:T(8,128)} %get-tuple-element.160, s32[]{:T(128)} %get-tuple-element.159, f32[8,8,256]{2,1,0:T(8,128)S(1)} %fusion.140, bf16[16,8,256,8,8]{2,4,3,1,0:T(8,128)(2,1)} %get-tuple-element.169, f32[8,256]{1,0:T(8,128)S(1)} %dynamic-slice_bitcast_fusion.2, ...), kind=kOutput, calls=%fused_computation.11.clone.1 | convolution fusion | flops 159400192 | bytes 3483648 | tf_op jit(solution)/shard_map/while/body/eval_jaxpr/shij,sjhd->sihd/dot_general | solution.py:44
  111.5 7.1 %fusion.140 = f32[8,8,256]{2,1,0:T(8,128)S(1)} fusion(f32[8,256]{1,0:T(8,128)S(1)} %dynamic-slice_bitcast_fusion.2, f32[8,256,256]{1,2,0:T(8,128)S(1)} %convert_element_type.231, bf16[16,8,256,8,8]{2,4,3,1,0:T(8,128)(2,1)} %get-tuple-element.171, s32[]{:T(128)} %get-tuple-element.159, bf16[16,8,256,8,8]{2,4,3,1,0:T(8,128)(2,1)} %get-tuple-element.170), kind=kOutput, calls=%fused_computation.121.clone.1 | convolution fusion | flops 88080640 | bytes 2696192 | tf_op jit(solution)/shard_map/while/body/eval_jaxpr/sub | solution.py:43
  118.6 9.0 %fusion.141 = f32[16,8,256,8,8]{2,4,3,1,0:T(8,128)} fusion(f32[16,8,256,8,8]{2,4,3,1,0:T(8,128)} %get-tuple-element.160, s32[]{:T(128)} %get-tuple-element.159, f32[8,8,256]{2,1,0:T(8,128)S(1)} %fusion.140, bf16[16,8,256,8,8]{2,4,3,1,0:T(8,128)(2,1)} %get-tuple-element.169, f32[8,256]{1,0:T(8,128)S(1)} %dynamic-slice_bitcast_fusion.2, ...), kind=kOutput, calls=%fused_computation.11.clone.1 | convolution fusion | flops 159400192 | bytes 3483648 | tf_op jit(solution)/shard_map/while/body/eval_jaxpr/shij,sjhd->sihd/dot_general | solution.py:44
  127.8 7.1 %fusion.140 = f32[8,8,256]{2,1,0:T(8,128)S(1)} fusion(f32[8,256]{1,0:T(8,128)S(1)} %dynamic-slice_bitcast_fusion.2, f32[8,256,256]{1,2,0:T(8,128)S(1)} %convert_element_type.231, bf16[16,8,256,8,8]{2,4,3,1,0:T(8,128)(2,1)} %get-tuple-element.171, s32[]{:T(128)} %get-tuple-element.159, bf16[16,8,256,8,8]{2,4,3,1,0:T(8,128)(2,1)} %get-tuple-element.170), kind=kOutput, calls=%fused_computation.121.clone.1 | convolution fusion | flops 88080640 | bytes 2696192 | tf_op jit(solution)/shard_map/while/body/eval_jaxpr/sub | solution.py:43
  135.0 8.9 %fusion.141 = f32[16,8,256,8,8]{2,4,3,1,0:T(8,128)} fusion(f32[16,8,256,8,8]{2,4,3,1,0:T(8,128)} %get-tuple-element.160, s32[]{:T(128)} %get-tuple-element.159, f32[8,8,256]{2,1,0:T(8,128)S(1)} %fusion.140, bf16[16,8,256,8,8]{2,4,3,1,0:T(8,128)(2,1)} %get-tuple-element.169, f32[8,256]{1,0:T(8,128)S(1)} %dynamic-slice_bitcast_fusion.2, ...), kind=kOutput, calls=%fused_computation.11.clone.1 | convolution fusion | flops 159400192 | bytes 3483648 | tf_op jit(solution)/shard_map/while/body/eval_jaxpr/shij,sjhd->sihd/dot_general | solution.py:44
  144.1 7.1 %fusion.140 = f32[8,8,256]{2,1,0:T(8,128)S(1)} fusion(f32[8,256]{1,0:T(8,128)S(1)} %dynamic-slice_bitcast_fusion.2, f32[8,256,256]{1,2,0:T(8,128)S(1)} %convert_element_type.231, bf16[16,8,256,8,8]{2,4,3,1,0:T(8,128)(2,1)} %get-tuple-element.171, s32[]{:T(128)} %get-tuple-element.159, bf16[16,8,256,8,8]{2,4,3,1,0:T(8,128)(2,1)} %get-tuple-element.170), kind=kOutput, calls=%fused_computation.121.clone.1 | convolution fusion | flops 88080640 | bytes 2696192 | tf_op jit(solution)/shard_map/while/body/eval_jaxpr/sub | solution.py:43
  151.2 9.0 %fusion.141 = f32[16,8,256,8,8]{2,4,3,1,0:T(8,128)} fusion(f32[16,8,256,8,8]{2,4,3,1,0:T(8,128)} %get-tuple-element.160, s32[]{:T(128)} %get-tuple-element.159, f32[8,8,256]{2,1,0:T(8,128)S(1)} %fusion.140, bf16[16,8,256,8,8]{2,4,3,1,0:T(8,128)(2,1)} %get-tuple-element.169, f32[8,256]{1,0:T(8,128)S(1)} %dynamic-slice_bitcast_fusion.2, ...), kind=kOutput, calls=%fused_computation.11.clone.1 | convolution fusion | flops 159400192 | bytes 3483648 | tf_op jit(solution)/shard_map/while/body/eval_jaxpr/shij,sjhd->sihd/dot_general | solution.py:44
  160.4 7.1 %fusion.140 = f32[8,8,256]{2,1,0:T(8,128)S(1)} fusion(f32[8,256]{1,0:T(8,128)S(1)} %dynamic-slice_bitcast_fusion.2, f32[8,256,256]{1,2,0:T(8,128)S(1)} %convert_element_type.231, bf16[16,8,256,8,8]{2,4,3,1,0:T(8,128)(2,1)} %get-tuple-element.171, s32[]{:T(128)} %get-tuple-element.159, bf16[16,8,256,8,8]{2,4,3,1,0:T(8,128)(2,1)} %get-tuple-element.170), kind=kOutput, calls=%fused_computation.121.clone.1 | convolution fusion | flops 88080640 | bytes 2696192 | tf_op jit(solution)/shard_map/while/body/eval_jaxpr/sub | solution.py:43
  167.5 8.9 %fusion.141 = f32[16,8,256,8,8]{2,4,3,1,0:T(8,128)} fusion(f32[16,8,256,8,8]{2,4,3,1,0:T(8,128)} %get-tuple-element.160, s32[]{:T(128)} %get-tuple-element.159, f32[8,8,256]{2,1,0:T(8,128)S(1)} %fusion.140, bf16[16,8,256,8,8]{2,4,3,1,0:T(8,128)(2,1)} %get-tuple-element.169, f32[8,256]{1,0:T(8,128)S(1)} %dynamic-slice_bitcast_fusion.2, ...), kind=kOutput, calls=%fused_computation.11.clone.1 | convolution fusion | flops 159400192 | bytes 3483648 | tf_op jit(solution)/shard_map/while/body/eval_jaxpr/shij,sjhd->sihd/dot_general | solution.py:44
  176.7 7.1 %fusion.140 = f32[8,8,256]{2,1,0:T(8,128)S(1)} fusion(f32[8,256]{1,0:T(8,128)S(1)} %dynamic-slice_bitcast_fusion.2, f32[8,256,256]{1,2,0:T(8,128)S(1)} %convert_element_type.231, bf16[16,8,256,8,8]{2,4,3,1,0:T(8,128)(2,1)} %get-tuple-element.171, s32[]{:T(128)} %get-tuple-element.159, bf16[16,8,256,8,8]{2,4,3,1,0:T(8,128)(2,1)} %get-tuple-element.170), kind=kOutput, calls=%fused_computation.121.clone.1 | convolution fusion | flops 88080640 | bytes 2696192 | tf_op jit(solution)/shard_map/while/body/eval_jaxpr/sub | solution.py:43
  183.8 9.0 %fusion.141 = f32[16,8,256,8,8]{2,4,3,1,0:T(8,128)} fusion(f32[16,8,256,8,8]{2,4,3,1,0:T(8,128)} %get-tuple-element.160, s32[]{:T(128)} %get-tuple-element.159, f32[8,8,256]{2,1,0:T(8,128)S(1)} %fusion.140, bf16[16,8,256,8,8]{2,4,3,1,0:T(8,128)(2,1)} %get-tuple-element.169, f32[8,256]{1,0:T(8,128)S(1)} %dynamic-slice_bitcast_fusion.2, ...), kind=kOutput, calls=%fused_computation.11.clone.1 | convolution fusion | flops 159400192 | bytes 3483648 | tf_op jit(solution)/shard_map/while/body/eval_jaxpr/shij,sjhd->sihd/dot_general | solution.py:44
  193.0 7.1 %fusion.140 = f32[8,8,256]{2,1,0:T(8,128)S(1)} fusion(f32[8,256]{1,0:T(8,128)S(1)} %dynamic-slice_bitcast_fusion.2, f32[8,256,256]{1,2,0:T(8,128)S(1)} %convert_element_type.231, bf16[16,8,256,8,8]{2,4,3,1,0:T(8,128)(2,1)} %get-tuple-element.171, s32[]{:T(128)} %get-tuple-element.159, bf16[16,8,256,8,8]{2,4,3,1,0:T(8,128)(2,1)} %get-tuple-element.170), kind=kOutput, calls=%fused_computation.121.clone.1 | convolution fusion | flops 88080640 | bytes 2696192 | tf_op jit(solution)/shard_map/while/body/eval_jaxpr/sub | solution.py:43
  200.1 8.9 %fusion.141 = f32[16,8,256,8,8]{2,4,3,1,0:T(8,128)} fusion(f32[16,8,256,8,8]{2,4,3,1,0:T(8,128)} %get-tuple-element.160, s32[]{:T(128)} %get-tuple-element.159, f32[8,8,256]{2,1,0:T(8,128)S(1)} %fusion.140, bf16[16,8,256,8,8]{2,4,3,1,0:T(8,128)(2,1)} %get-tuple-element.169, f32[8,256]{1,0:T(8,128)S(1)} %dynamic-slice_bitcast_fusion.2, ...), kind=kOutput, calls=%fused_computation.11.clone.1 | convolution fusion | flops 159400192 | bytes 3483648 | tf_op jit(solution)/shard_map/while/body/eval_jaxpr/shij,sjhd->sihd/dot_general | solution.py:44
  209.3 7.1 %fusion.140 = f32[8,8,256]{2,1,0:T(8,128)S(1)} fusion(f32[8,256]{1,0:T(8,128)S(1)} %dynamic-slice_bitcast_fusion.2, f32[8,256,256]{1,2,0:T(8,128)S(1)} %convert_element_type.231, bf16[16,8,256,8,8]{2,4,3,1,0:T(8,128)(2,1)} %get-tuple-element.171, s32[]{:T(128)} %get-tuple-element.159, bf16[16,8,256,8,8]{2,4,3,1,0:T(8,128)(2,1)} %get-tuple-element.170), kind=kOutput, calls=%fused_computation.121.clone.1 | convolution fusion | flops 88080640 | bytes 2696192 | tf_op jit(solution)/shard_map/while/body/eval_jaxpr/sub | solution.py:43
  216.4 9.0 %fusion.141 = f32[16,8,256,8,8]{2,4,3,1,0:T(8,128)} fusion(f32[16,8,256,8,8]{2,4,3,1,0:T(8,128)} %get-tuple-element.160, s32[]{:T(128)} %get-tuple-element.159, f32[8,8,256]{2,1,0:T(8,128)S(1)} %fusion.140, bf16[16,8,256,8,8]{2,4,3,1,0:T(8,128)(2,1)} %get-tuple-element.169, f32[8,256]{1,0:T(8,128)S(1)} %dynamic-slice_bitcast_fusion.2, ...), kind=kOutput, calls=%fused_computation.11.clone.1 | convolution fusion | flops 159400192 | bytes 3483648 | tf_op jit(solution)/shard_map/while/body/eval_jaxpr/shij,sjhd->sihd/dot_general | solution.py:44
  225.6 7.1 %fusion.140 = f32[8,8,256]{2,1,0:T(8,128)S(1)} fusion(f32[8,256]{1,0:T(8,128)S(1)} %dynamic-slice_bitcast_fusion.2, f32[8,256,256]{1,2,0:T(8,128)S(1)} %convert_element_type.231, bf16[16,8,256,8,8]{2,4,3,1,0:T(8,128)(2,1)} %get-tuple-element.171, s32[]{:T(128)} %get-tuple-element.159, bf16[16,8,256,8,8]{2,4,3,1,0:T(8,128)(2,1)} %get-tuple-element.170), kind=kOutput, calls=%fused_computation.121.clone.1 | convolution fusion | flops 88080640 | bytes 2696192 | tf_op jit(solution)/shard_map/while/body/eval_jaxpr/sub | solution.py:43
  232.7 9.0 %fusion.141 = f32[16,8,256,8,8]{2,4,3,1,0:T(8,128)} fusion(f32[16,8,256,8,8]{2,4,3,1,0:T(8,128)} %get-tuple-element.160, s32[]{:T(128)} %get-tuple-element.159, f32[8,8,256]{2,1,0:T(8,128)S(1)} %fusion.140, bf16[16,8,256,8,8]{2,4,3,1,0:T(8,128)(2,1)} %get-tuple-element.169, f32[8,256]{1,0:T(8,128)S(1)} %dynamic-slice_bitcast_fusion.2, ...), kind=kOutput, calls=%fused_computation.11.clone.1 | convolution fusion | flops 159400192 | bytes 3483648 | tf_op jit(solution)/shard_map/while/body/eval_jaxpr/shij,sjhd->sihd/dot_general | solution.py:44
  241.9 7.1 %fusion.140 = f32[8,8,256]{2,1,0:T(8,128)S(1)} fusion(f32[8,256]{1,0:T(8,128)S(1)} %dynamic-slice_bitcast_fusion.2, f32[8,256,256]{1,2,0:T(8,128)S(1)} %convert_element_type.231, bf16[16,8,256,8,8]{2,4,3,1,0:T(8,128)(2,1)} %get-tuple-element.171, s32[]{:T(128)} %get-tuple-element.159, bf16[16,8,256,8,8]{2,4,3,1,0:T(8,128)(2,1)} %get-tuple-element.170), kind=kOutput, calls=%fused_computation.121.clone.1 | convolution fusion | flops 88080640 | bytes 2696192 | tf_op jit(solution)/shard_map/while/body/eval_jaxpr/sub | solution.py:43
  249.0 9.0 %fusion.141 = f32[16,8,256,8,8]{2,4,3,1,0:T(8,128)} fusion(f32[16,8,256,8,8]{2,4,3,1,0:T(8,128)} %get-tuple-element.160, s32[]{:T(128)} %get-tuple-element.159, f32[8,8,256]{2,1,0:T(8,128)S(1)} %fusion.140, bf16[16,8,256,8,8]{2,4,3,1,0:T(8,128)(2,1)} %get-tuple-element.169, f32[8,256]{1,0:T(8,128)S(1)} %dynamic-slice_bitcast_fusion.2, ...), kind=kOutput, calls=%fused_computation.11.clone.1 | convolution fusion | flops 159400192 | bytes 3483648 | tf_op jit(solution)/shard_map/while/body/eval_jaxpr/shij,sjhd->sihd/dot_general | solution.py:44
  258.2 7.1 %fusion.140 = f32[8,8,256]{2,1,0:T(8,128)S(1)} fusion(f32[8,256]{1,0:T(8,128)S(1)} %dynamic-slice_bitcast_fusion.2, f32[8,256,256]{1,2,0:T(8,128)S(1)} %convert_element_type.231, bf16[16,8,256,8,8]{2,4,3,1,0:T(8,128)(2,1)} %get-tuple-element.171, s32[]{:T(128)} %get-tuple-element.159, bf16[16,8,256,8,8]{2,4,3,1,0:T(8,128)(2,1)} %get-tuple-element.170), kind=kOutput, calls=%fused_computation.121.clone.1 | convolution fusion | flops 88080640 | bytes 2696192 | tf_op jit(solution)/shard_map/while/body/eval_jaxpr/sub | solution.py:43
  265.3 9.0 %fusion.141 = f32[16,8,256,8,8]{2,4,3,1,0:T(8,128)} fusion(f32[16,8,256,8,8]{2,4,3,1,0:T(8,128)} %get-tuple-element.160, s32[]{:T(128)} %get-tuple-element.159, f32[8,8,256]{2,1,0:T(8,128)S(1)} %fusion.140, bf16[16,8,256,8,8]{2,4,3,1,0:T(8,128)(2,1)} %get-tuple-element.169, f32[8,256]{1,0:T(8,128)S(1)} %dynamic-slice_bitcast_fusion.2, ...), kind=kOutput, calls=%fused_computation.11.clone.1 | convolution fusion | flops 159400192 | bytes 3483648 | tf_op jit(solution)/shard_map/while/body/eval_jaxpr/shij,sjhd->sihd/dot_general | solution.py:44
  274.5 7.1 %fusion.140 = f32[8,8,256]{2,1,0:T(8,128)S(1)} fusion(f32[8,256]{1,0:T(8,128)S(1)} %dynamic-slice_bitcast_fusion.2, f32[8,256,256]{1,2,0:T(8,128)S(1)} %convert_element_type.231, bf16[16,8,256,8,8]{2,4,3,1,0:T(8,128)(2,1)} %get-tuple-element.171, s32[]{:T(128)} %get-tuple-element.159, bf16[16,8,256,8,8]{2,4,3,1,0:T(8,128)(2,1)} %get-tuple-element.170), kind=kOutput, calls=%fused_computation.121.clone.1 | convolution fusion | flops 88080640 | bytes 2696192 | tf_op jit(solution)/shard_map/while/body/eval_jaxpr/sub | solution.py:43
  281.6 9.0 %fusion.141 = f32[16,8,256,8,8]{2,4,3,1,0:T(8,128)} fusion(f32[16,8,256,8,8]{2,4,3,1,0:T(8,128)} %get-tuple-element.160, s32[]{:T(128)} %get-tuple-element.159, f32[8,8,256]{2,1,0:T(8,128)S(1)} %fusion.140, bf16[16,8,256,8,8]{2,4,3,1,0:T(8,128)(2,1)} %get-tuple-element.169, f32[8,256]{1,0:T(8,128)S(1)} %dynamic-slice_bitcast_fusion.2, ...), kind=kOutput, calls=%fused_computation.11.clone.1 | convolution fusion | flops 159400192 | bytes 3483648 | tf_op jit(solution)/shard_map/while/body/eval_jaxpr/shij,sjhd->sihd/dot_general | solution.py:44
  290.8 7.1 %fusion.140 = f32[8,8,256]{2,1,0:T(8,128)S(1)} fusion(f32[8,256]{1,0:T(8,128)S(1)} %dynamic-slice_bitcast_fusion.2, f32[8,256,256]{1,2,0:T(8,128)S(1)} %convert_element_type.231, bf16[16,8,256,8,8]{2,4,3,1,0:T(8,128)(2,1)} %get-tuple-element.171, s32[]{:T(128)} %get-tuple-element.159, bf16[16,8,256,8,8]{2,4,3,1,0:T(8,128)(2,1)} %get-tuple-element.170), kind=kOutput, calls=%fused_computation.121.clone.1 | convolution fusion | flops 88080640 | bytes 2696192 | tf_op jit(solution)/shard_map/while/body/eval_jaxpr/sub | solution.py:43
  297.9 8.9 %fusion.141 = f32[16,8,256,8,8]{2,4,3,1,0:T(8,128)} fusion(f32[16,8,256,8,8]{2,4,3,1,0:T(8,128)} %get-tuple-element.160, s32[]{:T(128)} %get-tuple-element.159, f32[8,8,256]{2,1,0:T(8,128)S(1)} %fusion.140, bf16[16,8,256,8,8]{2,4,3,1,0:T(8,128)(2,1)} %get-tuple-element.169, f32[8,256]{1,0:T(8,128)S(1)} %dynamic-slice_bitcast_fusion.2, ...), kind=kOutput, calls=%fused_computation.11.clone.1 | convolution fusion | flops 159400192 | bytes 3483648 | tf_op jit(solution)/shard_map/while/body/eval_jaxpr/shij,sjhd->sihd/dot_general | solution.py:44
  307.1 7.1 %fusion.140 = f32[8,8,256]{2,1,0:T(8,128)S(1)} fusion(f32[8,256]{1,0:T(8,128)S(1)} %dynamic-slice_bitcast_fusion.2, f32[8,256,256]{1,2,0:T(8,128)S(1)} %convert_element_type.231, bf16[16,8,256,8,8]{2,4,3,1,0:T(8,128)(2,1)} %get-tuple-element.171, s32[]{:T(128)} %get-tuple-element.159, bf16[16,8,256,8,8]{2,4,3,1,0:T(8,128)(2,1)} %get-tuple-element.170), kind=kOutput, calls=%fused_computation.121.clone.1 | convolution fusion | flops 88080640 | bytes 2696192 | tf_op jit(solution)/shard_map/while/body/eval_jaxpr/sub | solution.py:43
  314.2 9.0 %fusion.141 = f32[16,8,256,8,8]{2,4,3,1,0:T(8,128)} fusion(f32[16,8,256,8,8]{2,4,3,1,0:T(8,128)} %get-tuple-element.160, s32[]{:T(128)} %get-tuple-element.159, f32[8,8,256]{2,1,0:T(8,128)S(1)} %fusion.140, bf16[16,8,256,8,8]{2,4,3,1,0:T(8,128)(2,1)} %get-tuple-element.169, f32[8,256]{1,0:T(8,128)S(1)} %dynamic-slice_bitcast_fusion.2, ...), kind=kOutput, calls=%fused_computation.11.clone.1 | convolution fusion | flops 159400192 | bytes 3483648 | tf_op jit(solution)/shard_map/while/body/eval_jaxpr/shij,sjhd->sihd/dot_general | solution.py:44
  323.2 6.1 %fusion.64 = bf16[128,256,8,8]{1,3,2,0:T(8,128)(2,1)S(1)} fusion(f32[16,8,256,8,8]{2,4,3,1,0:T(8,128)} %get-tuple-element.42, bf16[4,128,256,8,8]{2,4,3,0,1:T(8,128)(2,1)} %convert_bitcast_fusion), kind=kLoop, calls=%fused_computation.60 | loop fusion | flops 12582912 | bytes 16777216 | tf_op jit(solution)/shard_map/convert_element_type | solution.py:48
  344.8 54.6 %all-reduce.3.cloned.1.call-done = f32[256,8,8]{2,1,0:T(8,128)} async-done(((f32[256,8,8]{2,1,0:T(8,128)}), f32[256,8,8]{2,1,0:T(8,128)}) %all-reduce.3.cloned.1.call-update) | async-done | bytes 65552 | tf_op jit(solution)/shard_map/psum | solution.py:65
  401.4 24.9 %pmax.7 = f32[256,8]{1,0:T(8,128)S(1)} all-reduce(f32[256,8]{1,0:T(8,128)S(1)} %get-tuple-element.104), channel_id=1, replica_groups=mesh['batch'=4,'seq'=8] {'seq'}, use_global_device_ids=true, to_apply=%region_14.15 | all-reduce | flops 2048 | bytes 16384 | tf_op jit(solution)/shard_map/pmax | solution.py:73
  428.7 6.0 %divide_bitcast_fusion = f32[128,256,8,8]{1,3,2,0:T(8,128)} fusion(bf16[128,256,144]{1,2,0:T(8,128)(2,1)} %copy-done.3), kind=kLoop, calls=%fused_computation.64 | loop fusion | flops 8388608 | bytes 12582912 | tf_op jit(solution)/shard_map/div | solution.py:48
  434.7 25.5 %psum.31 = f32[256,8]{1,0:T(8,128)S(1)} all-reduce(f32[256,8]{1,0:T(8,128)S(1)} %get-tuple-element.92), channel_id=1, replica_groups=mesh['batch'=4,'seq'=8] {'seq'}, use_global_device_ids=true, to_apply=%region_17.18 | all-reduce | flops 2048 | bytes 16384 | tf_op jit(solution)/shard_map/psum | solution.py:75
  460.1 24.8 %all-reduce.5.cloned.1.call-done = f32[256,8,8]{2,1,0:T(8,128)} async-done(((f32[256,8,8]{2,1,0:T(8,128)}), f32[256,8,8]{2,1,0:T(8,128)}) %all-reduce.5.cloned.1.call-update) | async-done | bytes 65552 | tf_op jit(solution)/shard_map/psum | solution.py:75
  486.9 8.5 %convert_reduce_fusion = (f32[128,256]{1,0:T(8,128)S(1)}, bf16[128,256,64]{1,2,0:T(8,128)(2,1)S(1)}) fusion(bf16[8,8,64]{2,1,0:T(8,128)(2,1)S(1)} %bitcast.136, f32[128,256,8,8]{1,3,2,0:T(8,128)} %divide_bitcast_fusion, f32[256,8,8]{0,1,2:T(8,128)S(1)} %copy.64, bf16[128,256,64]{1,2,0:T(8,128)(2,1)} %copy-done.1), kind=kOutput, calls=%fused_computation.36 | convolution fusion | flops 283082752 | bytes 16982016 | tf_op jit(solution)/shard_map/snhd,hdc->snc/dot_general | solution.py:78
  499.5 18.7 %fusion.63 = bf16[128,256,64]{1,2,0:T(8,128)(2,1)} fusion(bf16[128,256,64]{1,2,0:T(8,128)(2,1)} %copy-done.4, f32[128,256]{1,0:T(8,128)S(1)} %add_rsqrt_fusion, f32[128,256]{1,0:T(8,128)S(1)} %broadcast_multiply_fusion, bf16[256,64]{0,1:T(8,128)(2,1)S(1)} %copy-done.12, bf16[64,256]{1,0:T(8,128)(2,1)S(1)} %copy-done.13), kind=kOutput, calls=%fused_computation.58 | convolution fusion | flops 2178940928 | bytes 8716288 | tf_op jit(solution)/shard_map/snf,fc->snc/dot_general | solution.py:85
  518.2 7.3 %copy.67 = bf16[128,256,64]{0,2,1:T(8,128)(2,1)} copy(bf16[128,256,64]{1,2,0:T(8,128)(2,1)} %fusion.63) | data formatting | bytes 8388608 | tf_op jit(solution)/shard_map/convert_element_type | solution.py:86
  525.5 54.9 %all_to_all.18 = bf16[128,256,64]{0,2,1:T(8,128)(2,1)S(1)} all-to-all(bf16[128,256,64]{0,2,1:T(8,128)(2,1)} %copy.67), channel_id=1, replica_groups=mesh['batch'=4,'seq'=8] {'seq'}, dimensions={1} | all-to-all | bytes 8388608 | tf_op jit(solution)/shard_map/all_to_all | solution.py:98
  (101 shorter events, 45.0 us)
Async XLA Ops:
  6.5 326.6 %copy-start = (bf16[64,144]{1,0:T(8,128)(2,1)S(1)}, bf16[64,144]{1,0:T(8,128)(2,1)}, u32[]{:S(2)}) copy-start(bf16[64,144]{1,0:T(8,128)(2,1)} %param.18) | copy-start | bytes 55300
  6.6 10.4 %copy-start.5 = (s32[128,256]{1,0:T(8,128)S(1)}, s32[128,256]{1,0:T(8,128)}, u32[]{:S(2)}) copy-start(s32[128,256]{1,0:T(8,128)} %param.13) | copy-start | bytes 393220
  6.6 53.7 %all-gather.2.cloned.1.call-start = ((), (), s32[]{:S(2)}) async-start(), calls=%async_computation.1 | async-start | bytes 1179648 | tf_op jit(solution)/shard_map/all_gather | solution.py:93
  8.8 16.4 %copy-start.8 = (bf16[64,256]{1,0:T(8,128)(2,1)S(1)}, bf16[64,256]{1,0:T(8,128)(2,1)}, u32[]{:S(2)}) copy-start(bf16[64,256]{1,0:T(8,128)(2,1)} %param.16) | copy-start | bytes 98308
  16.9 382.5 %all-reduce.3.cloned.1.call-start = ((), (), s32[]{:S(2)}) async-start(), calls=%async_computation.2 | async-start | bytes 2097152 | tf_op jit(solution)/shard_map/psum | solution.py:65
  323.2 6.2 %copy-start.2 = (bf16[128,256,64]{1,2,0:T(8,128)(2,1)S(1)}, bf16[128,256,64]{1,2,0:T(8,128)(2,1)}, u32[]{:S(2)}) copy-start(bf16[128,256,64]{1,2,0:T(8,128)(2,1)} %param.12) | copy-start | bytes 12582916
  323.2 6.2 %copy-start.9 = (bf16[64,64]{1,0:T(8,128)(2,1)S(1)}, bf16[64,64]{1,0:T(8,128)(2,1)}, u32[]{:S(2)}) copy-start(bf16[64,64]{1,0:T(8,128)(2,1)} %param.17) | copy-start | bytes 24580
  331.0 5.0 copy-start.1
  331.1 8.6 %copy-start.6 = (f32[256,128]{0,1:T(8,128)S(1)}, f32[256,128]{0,1:T(8,128)}, u32[]{:S(2)}) copy-start(f32[256,128]{0,1:T(8,128)} %bitcast_convert_fusion) | copy-start | bytes 393220
  336.1 3.6 copy-start.3
  339.7 59.7 %copy-start.7 = (f32[128,256]{0,1:T(8,128)S(1)}, f32[128,256]{0,1:T(8,128)}, u32[]{:S(2)}) copy-start(f32[128,256]{0,1:T(8,128)} %copy.62) | copy-start | bytes 393220
  339.7 59.7 %copy-start.11 = (f32[256]{0:T(256)S(1)}, f32[256]{0:T(256)}, u32[]{:S(2)}) copy-start(f32[256]{0:T(256)} %broadcast_add_fusion) | copy-start | bytes 3076
  342.3 142.6 %all-reduce.5.cloned.1.call-start = ((), (), s32[]{:S(2)}) async-start(), calls=%async_computation.3 | async-start | bytes 2097152 | tf_op jit(solution)/shard_map/psum | solution.py:75
  428.6 58.2 %copy-start.10 = (bf16[64,64]{1,0:T(8,128)(2,1)S(1)}, bf16[64,64]{1,0:T(8,128)(2,1)}, u32[]{:S(2)}) copy-start(bf16[64,64]{1,0:T(8,128)(2,1)} %param.19) | copy-start | bytes 24580
  486.9 12.6 %copy-start.12 = (bf16[256,64]{0,1:T(8,128)(2,1)S(1)}, bf16[256,64]{0,1:T(8,128)(2,1)}, u32[]{:S(2)}) copy-start(bf16[256,64]{0,1:T(8,128)(2,1)} %param.21) | copy-start | bytes 98308
  486.9 12.6 %copy-start.13 = (bf16[64,256]{1,0:T(8,128)(2,1)S(1)}, bf16[64,256]{1,0:T(8,128)(2,1)}, u32[]{:S(2)}) copy-start(bf16[64,256]{1,0:T(8,128)(2,1)} %param.20) | copy-start | bytes 98308
  495.4 2.0 copy-start.4
Sparse Core Ops, SparseCore 0:
  17.0 24.5 all-gather.1
  342.4 56.9 all-reduce.2
  428.8 56.0 all-reduce.4
where the time goes:
time: 599 us; the launch traced here: 590 us
  matrix products  308 us (51%)
  blocking collectives  119 us (20%)
  waiting for transfers between devices  79.5 us (13%)
  other arithmetic  37.3 us (6%)
  local copies, waits for them, and re-layouts  31.8 us (5%)
  between operations  13.8 us (2%)
    dot_general x16, matrix products, tile_body(): jnp.einsum('shij,sjhd->sihd', attn_probs, v_tile, preferred_element_type=...  143 us
    sub x16, matrix products, tile_body(): attn_probs = jax.nn.softmax(logits, axis=-1).astype(jnp.bfloat16)  114 us
    all_to_all x1, blocking collectives, local_block(): return lax.all_to_all(after_trans, 'seq', 1, 0, tiled=True)  54.9 us
    psum x1, waiting for transfers between devices, column_attention(): q_sum, mask_count = lax.psum((q_sum, mask_count), 'seq')  54.6 us
    psum x1, blocking collectives, column_attention(): lax.psum((loc_den * rescale, loc_num * rescale[:, :, None]), 'seq')  25.5 us
    pmax x1, blocking collectives, column_attention(): glob_max = lax.pmax(loc_max, 'seq')  24.9 us
    psum x1, waiting for transfers between devices, column_attention(): lax.psum((loc_den * rescale, loc_num * rescale[:, :, None]), 'seq')  24.8 us
    dot_general x1, matrix products, transition(): jnp.einsum('snf,fc->snc', hidden, w_trans_out, preferred_element_type=jnp...  18.7 us
  transfers between devices with their start and end apart: 3, of which 2 were waited for; matrix products, arithmetic and copies ran while one was open for 6% of the time, Pallas kernels for 0%

commit v1 on v0

v1 whole, which is shorter than its diff:
```python
import functools

import jax
import jax.numpy as jnp
import numpy as np
from jax import lax
from jax.experimental import pallas as pl
from jax.experimental.pallas import tpu as pltpu
from jax.sharding import PartitionSpec as P

LN_EPS = 1.0e-5
MASK_BIG = 1.0e9
MEAN_EPS = 1.0e-10
LOG2E = 1.4426950408889634
BF = jnp.bfloat16
F32 = jnp.float32
MESH = pl.DeviceIdType.MESH

TILE_PAIRS = 8
LOOP_PAIRS = 2
HEADS_AHEAD = 4
NEXT_AT = 2
TILE_RES = 8


def layer_norm(x_in):
    x_f32 = x_in.astype(F32)
    mean_val = jnp.mean(x_f32, axis=-1, keepdims=True)
    centered = x_f32 - mean_val
    var_val = jnp.mean(centered * centered, axis=-1, keepdims=True)
    return (centered * lax.rsqrt(var_val + LN_EPS)).astype(BF)


def norm_rows(x):
    n = x.shape[0]
    mean = jnp.sum(x, axis=0, keepdims=True) * (1.0 / n)
    centered = x - mean
    var = jnp.sum(centered * centered, axis=0, keepdims=True) * (1.0 / n)
    return (centered * lax.rsqrt(var + LN_EPS)).astype(BF)


def dot(a, b):
    return lax.dot_general(a, b, (((1,), (0,)), ((), ())), preferred_element_type=F32)


def dot_nt(a, b):
    return lax.dot_general(a, b, (((1,), (1,)), ((), ())), preferred_element_type=F32)


def split_bf16(value, parts):
    out, rest = [], np.float64(value)
    for _ in range(parts):
        part = np.float64(np.asarray(rest, np.float32).astype(np.dtype(BF)))
        out.append(float(part))
        rest = rest - part
    return out


def row_prologue(x_bf, m_row, w_in_t, width, n_heads):
    head_dim = width // n_heads
    x = x_bf.astype(F32)
    proj = dot(w_in_t, norm_rows(x)).astype(BF)
    q = proj[:width].astype(F32) * (head_dim ** -0.5 * LOG2E)
    q_hi = q.astype(BF)
    q_lo = (q - q_hi.astype(F32)).astype(BF)
    k = proj[width:2 * width]
    v = proj[2 * width:3 * width].astype(F32)
    gate = jax.nn.sigmoid(proj[3 * width:].astype(F32))
    m_rows = jnp.broadcast_to(m_row - 1.0, (16, x.shape[1])).astype(BF)
    keys = jnp.concatenate([k, k, m_rows], axis=0).T
    return dict(x=x, q_hi=q_hi, q_lo=q_lo, v=v, gate=gate, keys=keys)


def row_stream(loads, w_in_t, w_out_t, bias_ref, n_heads, emit):
    width = w_out_t.shape[1]
    d = width // n_heads
    state = {}

    def start(i):
        if i < len(loads) and i not in state:
            state[i] = row_prologue(*loads[i](), w_in_t, width, n_heads)

    start(0)
    n_res = state[0]['x'].shape[1]
    mask_terms = split_bf16(MASK_BIG * LOG2E, 3)
    row_id = lax.broadcasted_iota(jnp.int32, (16, n_res), 0)
    mask_rows = jnp.zeros((16, n_res), F32)
    for n, term in enumerate(mask_terms):
        mask_rows = jnp.where(row_id == n, term, mask_rows)
    mask_rows = mask_rows.astype(BF)
    head_id = lax.broadcasted_iota(jnp.int32, (width, n_res), 0) // d
    zero = jnp.zeros((width, n_res), BF)
    ones = jnp.ones((8, n_res), F32)

    def logits(i, h):
        mine = head_id == h
        s = state[i]
        rhs = jnp.concatenate([jnp.where(mine, s['q_hi'], zero), jnp.where(mine, s['q_lo'], zero), mask_rows], axis=0)
        return dot(s['keys'], rhs) + bias_ref[h]

    items = [(i, h) for i in range(len(loads)) for h in range(n_heads)]
    pending, heads = {}, {}
    for step in range(len(items) + HEADS_AHEAD):
        if step < len(items):
            i, h = items[step]
            start(i)
            pending[step] = logits(i, h)
            if h == NEXT_AT:
                start(i + 1)
        if step >= HEADS_AHEAD:
            i, h = items[step - HEADS_AHEAD]
            s = state[i]
            t = pending.pop(step - HEADS_AHEAD)
            p = jnp.exp2(t - jnp.max(t, axis=0, keepdims=True)).astype(BF)
            lhs = jnp.concatenate([s['v'][h * d:(h + 1) * d], ones], axis=0).astype(BF)
            o = dot(lhs, p)
            heads.setdefault(i, []).append(o[:d] / o[d:d + 1])
            if h == n_heads - 1:
                gated = (s['gate'] * jnp.concatenate(heads.pop(i), axis=0)).astype(BF)
                emit(i, (s['x'] + dot(w_out_t, gated)).astype(BF))
                del state[i]


def row_kernel(n_dev, e_ref, m_ref, mt_ref, bias_ref, w_in_ref, w_out_ref, recv_ref, mrecv_ref,
               turned, outbox, send_sem, recv_sem, own_sem, msend_sem, mrecv_sem, mown_sem):
    t = pl.program_id(0)
    n_tiles = pl.num_programs(0)
    static_tiles = recv_sem.shape[0]
    me = lax.axis_index('seq')
    n_heads, _, n_res = bias_ref.shape
    pairs = e_ref.shape[1]
    share = n_res // n_dev
    n_local = mt_ref.shape[1]
    chans = turned.shape[1]

    def peer(k):
        return lax.rem(me + k, n_dev)

    def mask_copy(k):
        d = peer(k)
        return pltpu.make_async_remote_copy(
            src_ref=mt_ref.at[pl.ds(pl.multiple_of(d * share, share), share)],
            dst_ref=mrecv_ref.at[:, pl.ds(pl.multiple_of(me * n_local, n_local), n_local)],
            send_sem=msend_sem.at[k], recv_sem=mrecv_sem.at[k], device_id={'seq': d}, device_id_type=MESH)

    def mask_own():
        return pltpu.make_async_copy(
            mt_ref.at[pl.ds(pl.multiple_of(me * share, share), share)],
            mrecv_ref.at[:, pl.ds(pl.multiple_of(me * n_local, n_local), n_local)], mown_sem)

    def tile_copy(tile, k):
        d = peer(k)
        slot = lax.rem(tile, 2)
        return pltpu.make_async_remote_copy(
            src_ref=outbox.at[slot, pl.ds(d * share, share)],
            dst_ref=recv_ref.at[me, :, pl.ds(pl.multiple_of(tile * pairs, pairs), pairs), :],
            send_sem=send_sem.at[slot, k], recv_sem=recv_sem.at[tile, k], device_id={'seq': d}, device_id_type=MESH)

    def tile_own(tile):
        slot = lax.rem(tile, 2)
        return pltpu.make_async_copy(
            outbox.at[slot, pl.ds(me * share, share)],
            recv_ref.at[me, :, pl.ds(pl.multiple_of(tile * pairs, pairs), pairs), :], own_sem.at[slot])

    @pl.when(t == 0)
    def _():
        barrier = pltpu.get_barrier_semaphore()
        for k in range(1, n_dev):
            pl.semaphore_signal(barrier, inc=1, device_id={'seq': peer(k)}, device_id_type=MESH)
        pl.semaphore_wait(barrier, n_dev - 1)
        for k in range(1, n_dev):
            mask_copy(k).start()
        mask_own().start()

    w_in_t = w_in_ref[...]
    w_out_t = w_out_ref[...]

    def body(it, carry):
        def load(u):
            pair = it * LOOP_PAIRS + u // 2
            return lambda: (e_ref[u % 2, pair], m_ref[u % 2, pl.ds(pair, 1), :].astype(F32))

        done = {}

        def emit(u, e1):
            done[u] = e1.astype(F32)
            if u % 2:
                both = jnp.concatenate([done.pop(u - 1), done.pop(u)], axis=0).T
                turned[pl.ds(it * LOOP_PAIRS + u // 2, n_res, stride=pairs), :] = both

        row_stream([load(u) for u in range(2 * LOOP_PAIRS)], w_in_t, w_out_t, bias_ref, n_heads, emit)
        return carry

    lax.fori_loop(0, pairs // LOOP_PAIRS, body, 0)

    @pl.when(t >= 2)
    def _():
        for k in range(1, n_dev):
            tile_copy(t - 2, k).wait_send()
        tile_own(t - 2).wait()

    outbox[lax.rem(t, 2)] = turned[...].reshape(n_res, pairs, chans).astype(BF)
    for k in range(1, n_dev):
        tile_copy(t, k).start()
    tile_own(t).start()

    @pl.when(t == n_tiles - 1)
    def _():
        for tile in range(max(static_tiles - 2, 0), static_tiles):
            for k in range(1, n_dev):
                tile_copy(tile, k).wait_send()
            tile_own(tile).wait()
        for k in range(1, n_dev):
            mask_copy(k).wait_send()
            mask_copy(k).wait_recv()
        mask_own().wait()
        for tile in range(static_tiles):
            for k in range(1, n_dev):
                tile_copy(tile, k).wait_recv()


def row_attention(n_dev, e_t, mask, mask_t, bias_t, w_in_t, w_out_t):
    n_seq, chans, n_res = e_t.shape
    half = n_seq // 2
    tiles = half // TILE_PAIRS
    share = n_res // n_dev
    e_t = e_t.reshape(2, half, chans, n_res)
    mask = mask.reshape(2, half, n_res)

    def whole(a):
        return pl.BlockSpec(a.shape, lambda t: (0,) * a.ndim)

    return pl.pallas_call(
        functools.partial(row_kernel, n_dev),
        grid=(tiles,),
        in_specs=[
            pl.BlockSpec((2, TILE_PAIRS, chans, n_res), lambda t: (0, t, 0, 0)),
            pl.BlockSpec((2, TILE_PAIRS, n_res), lambda t: (0, t, 0)),
            whole(mask_t), whole(bias_t), whole(w_in_t), whole(w_out_t),
        ],
        out_specs=[pl.BlockSpec(memory_space=pl.ANY), pl.BlockSpec(memory_space=pl.ANY)],
        out_shape=[
            jax.ShapeDtypeStruct((n_dev, share, half, 2 * chans), BF),
            jax.ShapeDtypeStruct((share, n_dev * n_seq), F32),
        ],
        scratch_shapes=[
            pltpu.VMEM((n_res * TILE_PAIRS, 2 * chans), F32),
            pltpu.VMEM((2, n_res, TILE_PAIRS, 2 * chans), BF),
            pltpu.SemaphoreType.DMA((2, n_dev)),
            pltpu.SemaphoreType.DMA((tiles, n_dev)),
            pltpu.SemaphoreType.DMA((2,)),
            pltpu.SemaphoreType.DMA((n_dev,)),
            pltpu.SemaphoreType.DMA((n_dev,)),
            pltpu.SemaphoreType.DMA,
        ],
        compiler_params=pltpu.CompilerParams(
            dimension_semantics=('arbitrary',), vmem_limit_bytes=48 * 2 ** 20, collective_id=0, has_side_effects=True),
        name='row_attention',
    )(e_t, mask, mask_t, bias_t, w_in_t, w_out_t)


def col_kernel(n_heads, r_ref, m_ref, wc_ref, wco_ref, wti_ref, wto_ref, o_ref):
    n_dev, n_i, half, lanes = r_ref.shape
    chans = lanes // 2
    width = wco_ref.shape[1]
    d = width // n_heads
    eye = jnp.where(lax.broadcasted_iota(jnp.int32, (lanes, lanes), 0) == lax.broadcasted_iota(jnp.int32, (lanes, lanes), 1),
                    1.0, 0.0).astype(BF)
    low = lax.broadcasted_iota(jnp.int32, (chans, 2 * half), 1) < half
    same_head = (lax.broadcasted_iota(jnp.int32, (width, width), 0) // d
                 == lax.broadcasted_iota(jnp.int32, (width, width), 1) // d)
    state = {}

    def project(i):
        turned = dot_nt(eye, r_ref[:, i].reshape(n_dev * half, lanes))
        cols = []
        for n in range(n_dev // 2):
            a = turned[:chans, n * 2 * half:(n + 1) * 2 * half]
            b = turned[chans:, n * 2 * half:(n + 1) * 2 * half]
            cols.append(jnp.where(low, a, pltpu.roll(b, half, 1)))
            cols.append(jnp.where(low, pltpu.roll(a, half, 1), b))
        x = jnp.concatenate(cols, axis=1)
        state[i] = dict(x=x, proj=dot(wc_ref[...], norm_rows(x)).astype(BF))

    def attend(i):
        proj = state[i]['proj']
        m = m_ref[pl.ds(i, 1), :]
        q_sum = jnp.sum(proj[:width].astype(F32) * m, axis=1, keepdims=True)
        count = jnp.sum(m, axis=1, keepdims=True)
        q_mean = jnp.broadcast_to(q_sum / (count + MEAN_EPS), (width, width))
        q_rows = jnp.where(same_head, q_mean.T, 0.0).astype(BF)
        logits = dot(q_rows, proj[width:2 * width]) * (d ** -0.5) + MASK_BIG * (m - 1.0)
        e = jnp.exp(logits - jnp.max(logits, axis=1, keepdims=True))
        den = jnp.sum(e, axis=1, keepdims=True)
        num = jnp.sum(e * proj[2 * width:3 * width].astype(F32), axis=1, keepdims=True)
        gated = (jax.nn.sigmoid(proj[3 * width:].astype(F32)) * (num / den)).astype(BF)
        state[i]['e2'] = (state[i]['x'] + dot(wco_ref[...], gated)).astype(BF).astype(F32)

    def transition(i):
        e2 = state.pop(i)['e2']
        hidden = jnp.maximum(dot(wti_ref[...], norm_rows(e2)), 0.0).astype(BF)
        o_ref[i] = (e2 + dot(wto_ref[...], hidden)).astype(BF)

    for step in range(n_i + 2):
        if step < n_i:
            project(step)
        if 0 <= step - 1 < n_i:
            attend(step - 1)
        if step >= 2:
            transition(step - 2)


def column_and_transition(n_heads, received, mask, wc, wco, wti, wto):
    n_dev, share, half, lanes = received.shape
    n_seq = mask.shape[1]

    def whole(a):
        return pl.BlockSpec(a.shape, lambda n: (0,) * a.ndim)

    return pl.pallas_call(
        functools.partial(col_kernel, n_heads),
        grid=(share // TILE_RES,),
        in_specs=[
            pl.BlockSpec((n_dev, TILE_RES, half, lanes), lambda n: (0, n, 0, 0)),
            pl.BlockSpec((TILE_RES, n_seq), lambda n: (n, 0)),
            whole(wc), whole(wco), whole(wti), whole(wto),
        ],
        out_specs=pl.BlockSpec((TILE_RES, lanes // 2, n_seq), lambda n: (n, 0, 0)),
        out_shape=jax.ShapeDtypeStruct((share, lanes // 2, n_seq), BF),
        compiler_params=pltpu.CompilerParams(dimension_semantics=('arbitrary',), vmem_limit_bytes=48 * 2 ** 20),
        name='column_and_transition',
    )(received, mask, wc, wco, wti, wto)


def column_weights(w_col_in, width, n_heads):
    d = width // n_heads
    w_t = w_col_in.T
    k = jnp.tile(w_t[width:width + d], (n_heads, 1))
    v = jnp.tile(w_t[width + d:width + 2 * d], (n_heads, 1))
    return jnp.concatenate([w_t[:width], k, v, w_t[width + 2 * d:]], axis=0)


def solution(mesh):
    n_dev = mesh.shape['seq']

    def local_block(msa, mask, pair, w_pair_bias, w_row_in, w_row_out, w_col_in, w_col_out, w_trans_in, w_trans_out):
        n_heads = w_pair_bias.shape[1]
        width = w_col_out.shape[0]
        bias_rows = jnp.einsum('ijc,ch->hij', layer_norm(pair), w_pair_bias, preferred_element_type=F32).astype(BF)
        bias_full = lax.all_gather(bias_rows, 'seq', axis=1, tiled=True)
        bias_t = jnp.transpose(bias_full, (0, 2, 1)).astype(F32) * LOG2E
        received, mask_cols = row_attention(
            n_dev, jnp.transpose(msa, (0, 2, 1)), mask, mask.T.astype(F32), bias_t, w_row_in.T, w_row_out.T)
        out = column_and_transition(
            n_heads, received, mask_cols, column_weights(w_col_in, width, n_heads), w_col_out.T, w_trans_in.T, w_trans_out.T)
        return jnp.transpose(out, (2, 0, 1))

    rows = P(('batch', 'seq'))
    return jax.shard_map(local_block, mesh=mesh, in_specs=(rows, rows, rows) + (P(),) * 7, out_specs=P('batch', 'seq'),
                         check_vma=False)
```

time: 599 us -> 208 us (0.35); the launches traced: 590 us -> 208 us
  matrix products: 308 us -> 3.55 us
  Pallas kernels: 0 us -> 156 us
  blocking collectives: 119 us -> 0 us
  waiting for transfers between devices: 79.5 us -> 24 us
  other arithmetic: 37.3 us -> 6.19 us
  local copies, waits for them, and re-layouts: 31.8 us -> 4.46 us
    dot_general x24 -> x1, matrix products: 193 us -> 3.55 us  [local_block(): jnp.einsum('ijc,ch->hij', layer_norm(pair), w_pair_bias, preferred_elemen...]
    pallas_call x0 -> x2, Pallas kernels: none -> 156 us  [the longest x1 117 us: row_attention(): pl.pallas_call(functools.partial(row_kernel, n_dev), grid=(tiles,), in_sp...]
    sub x16 -> x0, matrix products: 114 us -> none  [tile_body(): attn_probs = jax.nn.softmax(logits, axis=-1).astype(jnp.bfloat16)]
    psum x2 -> x0, waiting for transfers between devices: 79.4 us -> none  [the longest x1 54.6 us: column_attention(): q_sum, mask_count = lax.psum((q_sum, mask_count), 'seq')]
    all_to_all x1 -> x0, blocking collectives: 54.9 us -> none  [local_block(): return lax.all_to_all(after_trans, 'seq', 1, 0, tiled=True)]
    psum x2 -> x0, blocking collectives: 39.7 us -> none  [the longest x1 25.5 us: column_attention(): lax.psum((loc_den * rescale, loc_num * rescale[:, :, None]), 'seq')]
    pmax x1 -> x0, blocking collectives: 24.9 us -> none  [column_attention(): glob_max = lax.pmax(loc_max, 'seq')]
    all_gather x1, waiting for transfers between devices: 0.01 us -> 23.9 us  [local_block(): bias_full = lax.all_gather(bias_rows, 'seq', axis=1, tiled=True)]
  transfers between devices with their start and end apart: 3 -> 1, of which waited for: 2 -> 1; matrix products, arithmetic and copies ran while one was open for 6% -> 0% of each run, Pallas kernels for 0% -> 0%
where the time goes in v1:
time: 208 us
  Pallas kernels  156 us (75%)
  waiting for transfers between devices  24 us (12%)
  between operations  13.7 us (7%)
  other arithmetic  6.19 us (3%)
  local copies, waits for them, and re-layouts  4.46 us (2%)
  matrix products  3.55 us (2%)
    pallas_call x1, Pallas kernels, row_attention(): pl.pallas_call(functools.partial(row_kernel, n_dev), grid=(tiles,), in_sp...  117 us
    pallas_call x1, Pallas kernels, column_and_transition(): pl.pallas_call(functools.partial(col_kernel, n_heads), grid=(share // TIL...  38.7 us
    all_gather x1, waiting for transfers between devices, local_block(): bias_full = lax.all_gather(bias_rows, 'seq', axis=1, tiled=True)  23.9 us
  transfers between devices with their start and end apart: 1, of which 1 were waited for; matrix products, arithmetic and copies ran while one was open for 0% of the time, Pallas kernels for 0%

profile of v1, /device:TPU:81, one launch (start us, length us, event | category | flops | bytes accessed | tf_op | source)
XLA Modules:
  0.0 207.6 jit_solution(12328936704782384213)
XLA Ops:
  6.5 0.0 copy-start
  6.6 0.0 copy-start.4
  6.6 0.0 copy-start.8
  6.6 0.0 copy-start.9
  6.6 0.0 copy-start.7
  6.6 0.0 copy-start.5
  6.6 0.0 copy-start.6
  6.6 0.0 copy-start.2
  6.6 0.1 all-gather.2.cloned.1.call-start
  6.7 2.3 %convert_reduce_fusion = f32[32,256]{1,0:T(8,128)S(1)} fusion(bf16[32,256,128]{2,1,0:T(8,128)(2,1)} %param.12), kind=kLoop, calls=%fused_computation.1 | loop fusion | flops 2088960 | bytes 2129920 | tf_op jit(solution)/shard_map/reduce_sum | solution.py:28
  9.0 3.6 %fusion.2 = f32[32,256]{1,0:T(8,128)S(1)} fusion(bf16[32,256,128]{2,1,0:T(8,128)(2,1)} %param.12, f32[32,256]{1,0:T(8,128)S(1)} %broadcast_multiply_fusion), kind=kLoop, calls=%fused_computation.4 | loop fusion | flops 4186112 | bytes 2162688 | tf_op jit(solution)/shard_map/reduce_sum | solution.py:30
  12.6 0.0 copy-done
  12.6 0.0 copy-done.4
  12.7 3.5 %fusion.11 = bf16[8,32,256]{2,0,1:T(8,128)(2,1)} fusion(bf16[32,256,128]{2,1,0:T(8,128)(2,1)S(1)} %copy-done.4, f32[32,256]{1,0:T(8,128)S(1)} %add_rsqrt_fusion, f32[32,256]{1,0:T(8,128)S(1)} %broadcast_multiply_fusion, bf16[128,8]{0,1:T(8,128)(2,1)S(1)} %copy-done), kind=kOutput, calls=%fused_computation.11 | convolution fusion | flops 21037056 | bytes 2295808 | tf_op jit(solution)/shard_map/ijc,ch->hij/dot_general | solution.py:349
  16.2 0.1 all-gather.2.cloned.1.call-update
  16.3 0.0 copy-done.8
  16.3 0.1 copy.21
  16.4 0.0 copy-done.9
  16.4 0.1 copy.23
  16.5 0.0 copy-done.7
  16.5 0.1 copy.22
  16.6 0.0 copy-done.5
  16.6 0.1 copy.20
  16.7 0.0 copy-done.6
  16.7 0.1 copy.24
  16.9 0.0 copy-done.2
  16.9 0.1 copy.18
  17.0 23.9 %all-gather.2.cloned.1.call-done = bf16[8,256,256]{2,0,1:T(8,128)(2,1)} async-done(((bf16[8,32,256]{2,0,1:T(8,128)(2,1)}), bf16[8,256,256]{2,0,1:T(8,128)(2,1)}) %all-gather.2.cloned.1.call-update) | async-done | bytes 1048592 | tf_op jit(solution)/shard_map/all_gather | solution.py:350
  40.9 1.6 copy.19
  42.6 0.0 copy-start.3
  42.6 0.2 multiply_bitcast_fusion.bias_ref
  42.8 117.0 %row_attention.1 = (bf16[8,32,64,128]{3,2,1,0:T(8,128)(2,1)}, f32[32,1024]{1,0:T(8,128)S(1)}) custom-call(bf16[2,64,64,256]{3,2,1,0:T(8,128)(2,1)} %bitcast.30, s32[2,64,256]{2,1,0:T(8,128)S(1)} %bitcast.24, f32[256,128]{1,0:T(8,128)S(1)} %convert_bitcast_fusion.mt_ref, f32[8,256,256]{2,1,0:T(8,128)S(1)} %multiply_bitcast_fusion.bias_ref, ...), custom_call_target="tpu_custom_call" | custom-call | tf_op jit(solution)/shard_map/row_attention/pallas_call | solution.py:233
  159.8 0.0 copy-done.3
  159.8 0.0 copy-start.1
  159.8 2.2 %copy-done.1 = bf16[8,32,64,128]{3,2,1,0:T(8,128)(2,1)S(1)} copy-done((bf16[8,32,64,128]{3,2,1,0:T(8,128)(2,1)S(1)}, bf16[8,32,64,128]{3,2,1,0:T(8,128)(2,1)}, u32[]{:S(2)}) %copy-start.1) | copy-done | bytes 4194328
  162.0 38.7 %column_and_transition.1 = bf16[32,64,1024]{2,1,0:T(8,128)(2,1)} custom-call(bf16[8,32,64,128]{3,2,1,0:T(8,128)(2,1)S(1)} %copy-done.1, f32[32,1024]{1,0:T(8,128)S(1)} %get-tuple-element.8.m_ref, bf16[256,64]{1,0:T(8,128)(2,1)S(1)} %pad_maximum_fusion.wc_ref, bf16[64,64]{1,0:T(8,128)(2,1)S(1)} %bitcast.27, bf16[256,64]{1,0:T(8,128)(2,1)S(1)} %bitcast.25, ...), custom_call_target="tpu_custom_call" | custom-call | tf_op jit(solution)/shard_map/column_and_transition/pallas_call | solution.py:320
  (7 shorter events, 0.1 us)
Async XLA Ops:
  6.5 6.1 %copy-start = (bf16[128,8]{0,1:T(8,128)(2,1)S(1)}, bf16[128,8]{0,1:T(8,128)(2,1)}, u32[]{:S(2)}) copy-start(bf16[128,8]{0,1:T(8,128)(2,1)} %param.13) | copy-start | bytes 6148
  6.6 6.1 %copy-start.4 = (bf16[32,256,128]{2,1,0:T(8,128)(2,1)S(1)}, bf16[32,256,128]{2,1,0:T(8,128)(2,1)}, u32[]{:S(2)}) copy-start(bf16[32,256,128]{2,1,0:T(8,128)(2,1)} %param.12) | copy-start | bytes 6291460
  6.6 9.7 %copy-start.8 = (bf16[64,64]{1,0:T(8,128)(2,1)S(1)}, bf16[64,64]{1,0:T(8,128)(2,1)}, u32[]{:S(2)}) copy-start(bf16[64,64]{1,0:T(8,128)(2,1)} %param.15) | copy-start | bytes 24580
  6.6 9.8 %copy-start.9 = (bf16[64,64]{1,0:T(8,128)(2,1)S(1)}, bf16[64,64]{1,0:T(8,128)(2,1)}, u32[]{:S(2)}) copy-start(bf16[64,64]{1,0:T(8,128)(2,1)} %param.17) | copy-start | bytes 24580
  6.6 9.9 %copy-start.7 = (bf16[64,144]{1,0:T(8,128)(2,1)S(1)}, bf16[64,144]{1,0:T(8,128)(2,1)}, u32[]{:S(2)}) copy-start(bf16[64,144]{1,0:T(8,128)(2,1)} %param.16) | copy-start | bytes 55300
  6.6 10.0 %copy-start.5 = (bf16[64,256]{1,0:T(8,128)(2,1)S(1)}, bf16[64,256]{1,0:T(8,128)(2,1)}, u32[]{:S(2)}) copy-start(bf16[64,256]{1,0:T(8,128)(2,1)} %param.14) | copy-start | bytes 98308
  6.6 10.2 %copy-start.6 = (bf16[64,256]{1,0:T(8,128)(2,1)S(1)}, bf16[64,256]{1,0:T(8,128)(2,1)}, u32[]{:S(2)}) copy-start(bf16[64,256]{1,0:T(8,128)(2,1)} %param.18) | copy-start | bytes 98308
  6.6 10.3 %copy-start.2 = (s32[128,256]{1,0:T(8,128)S(1)}, s32[128,256]{1,0:T(8,128)}, u32[]{:S(2)}) copy-start(s32[128,256]{1,0:T(8,128)} %param.11) | copy-start | bytes 393220
  6.6 34.4 %all-gather.2.cloned.1.call-start = ((), (), s32[]{:S(2)}) async-start(), calls=%async_computation | async-start | bytes 1179648 | tf_op jit(solution)/shard_map/all_gather | solution.py:350
  42.6 117.2 %copy-start.3 = (bf16[256,64]{0,1:T(8,128)(2,1)S(1)}, bf16[256,64]{0,1:T(8,128)(2,1)}, u32[]{:S(2)}) copy-start(bf16[256,64]{0,1:T(8,128)(2,1)} %param.19) | copy-start | bytes 98308
  159.8 2.2 %copy-start.1 = (bf16[8,32,64,128]{3,2,1,0:T(8,128)(2,1)S(1)}, bf16[8,32,64,128]{3,2,1,0:T(8,128)(2,1)}, u32[]{:S(2)}) copy-start(bf16[8,32,64,128]{3,2,1,0:T(8,128)(2,1)} %get-tuple-element.7.r_ref) | copy-start | bytes 12582916
Sparse Core Ops, SparseCore 0:
  16.4 24.5 all-gather.1

commit v2 on v1

--- a/solution.py
+++ b/solution.py
@@ -17,18 +17,11 @@
 MESH = pl.DeviceIdType.MESH
 
 TILE_PAIRS = 8
-LOOP_PAIRS = 2
-HEADS_AHEAD = 4
+LOOP_PAIRS = 8
+HEADS_AHEAD = 5
 NEXT_AT = 2
 TILE_RES = 8
-
-
-def layer_norm(x_in):
-    x_f32 = x_in.astype(F32)
-    mean_val = jnp.mean(x_f32, axis=-1, keepdims=True)
-    centered = x_f32 - mean_val
-    var_val = jnp.mean(centered * centered, axis=-1, keepdims=True)
-    return (centered * lax.rsqrt(var_val + LN_EPS)).astype(BF)
+BIAS_ROWS = 16
 
 
 def norm_rows(x):
@@ -88,14 +81,19 @@
     for n, term in enumerate(mask_terms):
         mask_rows = jnp.where(row_id == n, term, mask_rows)
     mask_rows = mask_rows.astype(BF)
-    head_id = lax.broadcasted_iota(jnp.int32, (width, n_res), 0) // d
-    zero = jnp.zeros((width, n_res), BF)
+    per_tile = 16 // d
+    sub_id = lax.broadcasted_iota(jnp.int32, (16, n_res), 0) // d
+    zero = jnp.zeros((16, n_res), BF)
     ones = jnp.ones((8, n_res), F32)
 
+    def only_head(q, h):
+        mine = h // per_tile
+        own = jnp.where(sub_id == h % per_tile, q[mine * 16:(mine + 1) * 16], zero)
+        return [own if n == mine else zero for n in range(width // 16)]
+
     def logits(i, h):
-        mine = head_id == h
         s = state[i]
-        rhs = jnp.concatenate([jnp.where(mine, s['q_hi'], zero), jnp.where(mine, s['q_lo'], zero), mask_rows], axis=0)
+        rhs = jnp.concatenate(only_head(s['q_hi'], h) + only_head(s['q_lo'], h) + [mask_rows], axis=0)
         return dot(s['keys'], rhs) + bias_ref[h]
 
     items = [(i, h) for i in range(len(loads)) for h in range(n_heads)]
@@ -121,8 +119,9 @@
                 del state[i]
 
 
-def row_kernel(n_dev, e_ref, m_ref, mt_ref, bias_ref, w_in_ref, w_out_ref, recv_ref, mrecv_ref,
-               turned, outbox, send_sem, recv_sem, own_sem, msend_sem, mrecv_sem, mown_sem):
+def row_kernel(n_dev, e_ref, m_ref, mt_ref, z_ref, w_pair_ref, w_in_ref, w_out_ref, recv_ref, mrecv_ref,
+               turned, outbox, bias_rows, bias_all, bias_ref, send_sem, recv_sem, own_sem, msend_sem, mrecv_sem, mown_sem,
+               bsend_sem, brecv_sem):
     t = pl.program_id(0)
     n_tiles = pl.num_programs(0)
     static_tiles = recv_sem.shape[0]
@@ -162,15 +161,56 @@
             outbox.at[slot, pl.ds(me * share, share)],
             recv_ref.at[me, :, pl.ds(pl.multiple_of(tile * pairs, pairs), pairs), :], own_sem.at[slot])
 
+    def bias_copy(c, k):
+        rows = bias_all.at[:, pl.ds(pl.multiple_of(me * share + c * BIAS_ROWS, BIAS_ROWS), BIAS_ROWS), :]
+        return pltpu.make_async_remote_copy(
+            src_ref=rows, dst_ref=rows, send_sem=bsend_sem.at[c, k], recv_sem=brecv_sem.at[c, k],
+            device_id={'seq': peer(k)}, device_id_type=MESH)
+
     @pl.when(t == 0)
     def _():
         barrier = pltpu.get_barrier_semaphore()
         for k in range(1, n_dev):
             pl.semaphore_signal(barrier, inc=1, device_id={'seq': peer(k)}, device_id_type=MESH)
-        pl.semaphore_wait(barrier, n_dev - 1)
+        z_ch = z_ref.shape[2]
+        eye = jnp.where(lax.broadcasted_iota(jnp.int32, (z_ch, z_ch), 0) == lax.broadcasted_iota(jnp.int32, (z_ch, z_ch), 1),
+                        1.0, 0.0).astype(BF)
+        w_pair = w_pair_ref[...]
+        for c in range(share // BIAS_ROWS):
+            def rows_step(n, carry, c=c):
+                i = c * BIAS_ROWS + n * 4
+                turned_z = dot_nt(eye, z_ref[pl.ds(i, 4)].reshape(4 * n_res, z_ch))
+                b = dot(w_pair, norm_rows(turned_z))
+                for u in range(4):
+                    for part in range(n_res // 128):
+                        at = u * n_res + part * 128
+                        bias_rows[part, pl.ds(i + u, n_heads, stride=share), :] = b[:, at:at + 128]
+                return carry
+
+            lax.fori_loop(0, BIAS_ROWS // 4, rows_step, 0)
+            for part in range(n_res // 128):
+                own = bias_rows[part].reshape(n_heads, share, 128)[:, c * BIAS_ROWS:(c + 1) * BIAS_ROWS]
+                bias_all[:, pl.ds(pl.multiple_of(me * share + c * BIAS_ROWS, BIAS_ROWS), BIAS_ROWS),
+                         part * 128:(part + 1) * 128] = own.astype(BF)
+            if c == 0:
+                pl.semaphore_wait(barrier, n_dev - 1)
+            for k in range(1, n_dev):
+                bias_copy(c, k).start()
         for k in range(1, n_dev):
             mask_copy(k).start()
         mask_own().start()
+        for c in range(share // BIAS_ROWS):
+            for k in range(1, n_dev):
+                bias_copy(c, k).wait_recv()
+
+        def turn(h, carry):
+            bias_ref[h] = bias_all[h].astype(F32).T * LOG2E
+            return carry
+
+        lax.fori_loop(0, n_heads, turn, 0)
+        for c in range(share // BIAS_ROWS):
+            for k in range(1, n_dev):
+                bias_copy(c, k).wait_send()
 
     w_in_t = w_in_ref[...]
     w_out_t = w_out_ref[...]
@@ -219,11 +259,12 @@
                 tile_copy(tile, k).wait_recv()
 
 
-def row_attention(n_dev, e_t, mask, mask_t, bias_t, w_in_t, w_out_t):
+def row_attention(n_dev, e_t, mask, mask_t, pair, w_pair_t, w_in_t, w_out_t):
     n_seq, chans, n_res = e_t.shape
     half = n_seq // 2
     tiles = half // TILE_PAIRS
     share = n_res // n_dev
+    n_heads = w_pair_t.shape[0]
     e_t = e_t.reshape(2, half, chans, n_res)
     mask = mask.reshape(2, half, n_res)
 
@@ -236,7 +277,7 @@
         in_specs=[
             pl.BlockSpec((2, TILE_PAIRS, chans, n_res), lambda t: (0, t, 0, 0)),
             pl.BlockSpec((2, TILE_PAIRS, n_res), lambda t: (0, t, 0)),
-            whole(mask_t), whole(bias_t), whole(w_in_t), whole(w_out_t),
+            whole(mask_t), whole(pair), whole(w_pair_t), whole(w_in_t), whole(w_out_t),
         ],
         out_specs=[pl.BlockSpec(memory_space=pl.ANY), pl.BlockSpec(memory_space=pl.ANY)],
         out_shape=[
@@ -246,17 +287,22 @@
         scratch_shapes=[
             pltpu.VMEM((n_res * TILE_PAIRS, 2 * chans), F32),
             pltpu.VMEM((2, n_res, TILE_PAIRS, 2 * chans), BF),
+            pltpu.VMEM((n_res // 128, n_heads * share, 128), F32),
+            pltpu.VMEM((n_heads, n_res, n_res), BF),
+            pltpu.VMEM((n_heads, n_res, n_res), F32),
             pltpu.SemaphoreType.DMA((2, n_dev)),
             pltpu.SemaphoreType.DMA((tiles, n_dev)),
             pltpu.SemaphoreType.DMA((2,)),
             pltpu.SemaphoreType.DMA((n_dev,)),
             pltpu.SemaphoreType.DMA((n_dev,)),
             pltpu.SemaphoreType.DMA,
+            pltpu.SemaphoreType.DMA((share // BIAS_ROWS, n_dev)),
+            pltpu.SemaphoreType.DMA((share // BIAS_ROWS, n_dev)),
         ],
         compiler_params=pltpu.CompilerParams(
             dimension_semantics=('arbitrary',), vmem_limit_bytes=48 * 2 ** 20, collective_id=0, has_side_effects=True),
         name='row_attention',
-    )(e_t, mask, mask_t, bias_t, w_in_t, w_out_t)
+    )(e_t, mask, mask_t, pair, w_pair_t, w_in_t, w_out_t)
 
 
 def col_kernel(n_heads, r_ref, m_ref, wc_ref, wco_ref, wti_ref, wto_ref, o_ref):
@@ -346,11 +392,8 @@
     def local_block(msa, mask, pair, w_pair_bias, w_row_in, w_row_out, w_col_in, w_col_out, w_trans_in, w_trans_out):
         n_heads = w_pair_bias.shape[1]
         width = w_col_out.shape[0]
-        bias_rows = jnp.einsum('ijc,ch->hij', layer_norm(pair), w_pair_bias, preferred_element_type=F32).astype(BF)
-        bias_full = lax.all_gather(bias_rows, 'seq', axis=1, tiled=True)
-        bias_t = jnp.transpose(bias_full, (0, 2, 1)).astype(F32) * LOG2E
         received, mask_cols = row_attention(
-            n_dev, jnp.transpose(msa, (0, 2, 1)), mask, mask.T.astype(F32), bias_t, w_row_in.T, w_row_out.T)
+            n_dev, jnp.transpose(msa, (0, 2, 1)), mask, mask.T.astype(F32), pair, w_pair_bias.T, w_row_in.T, w_row_out.T)
         out = column_and_transition(
             n_heads, received, mask_cols, column_weights(w_col_in, width, n_heads), w_col_out.T, w_trans_in.T, w_trans_out.T)
         return jnp.transpose(out, (2, 0, 1))

time: 208 us -> 158 us (0.76)
  waiting for transfers between devices: 24 us -> 0 us
  between operations: 13.7 us -> 0.1 us
  Pallas kernels: 156 us -> 147 us
  other arithmetic: 6.19 us -> 0.03 us
  local copies, waits for them, and re-layouts: 4.46 us -> 10.6 us
  matrix products: 3.55 us -> 0 us
    all_gather x1 -> x0, waiting for transfers between devices: 23.9 us -> none  [local_block(): bias_full = lax.all_gather(bias_rows, 'seq', axis=1, tiled=True)]
    pallas_call x1, Pallas kernels: 117 us -> 108 us  [row_attention(): pl.pallas_call(functools.partial(row_kernel, n_dev), grid=(tiles,), in_sp...]
    unnamed x26 -> x16, local copies, waits for them, and re-layouts: 2.82 us -> 10.6 us
    reduce_sum x2 -> x0, other arithmetic: 5.93 us -> none  [the longest x1 3.58 us: layer_norm(): var_val = jnp.mean(centered * centered, axis=-1, keepdims=True)]
    dot_general x1 -> x0, matrix products: 3.55 us -> none  [local_block(): jnp.einsum('ijc,ch->hij', layer_norm(pair), w_pair_bias, preferred_elemen...]
  transfers between devices with their start and end apart: 1 -> 0, of which waited for: 1 -> 0; matrix products, arithmetic and copies ran while one was open for 0% -> 0% of each run, Pallas kernels for 0% -> 0%
where the time goes in v2:
time: 158 us; the launch traced here: 157 us
  Pallas kernels  147 us (93%)
  local copies, waits for them, and re-layouts  10.6 us (7%)
    pallas_call x1, Pallas kernels, row_attention(): pl.pallas_call(functools.partial(row_kernel, n_dev), grid=(tiles,), in_sp...  108 us
    pallas_call x1, Pallas kernels, column_and_transition(): pl.pallas_call(functools.partial(col_kernel, n_heads), grid=(share // TIL...  38.6 us
    unnamed x16, local copies, waits for them, and re-layouts  10.6 us

profile of v2, /device:TPU:81, one launch (start us, length us, event | category | flops | bytes accessed | tf_op | source)
XLA Modules:
  0.0 157.4 jit_solution(10138814416434346838)
XLA Ops:
  0.0 0.0 copy-start.3
  0.0 0.8 copy.13
  0.8 0.8 copy.15
  1.6 0.9 copy.14
  2.6 0.9 copy.12
  3.4 0.9 copy.16
  4.3 1.0 copy.11
  5.3 0.0 copy-start.1
  5.4 1.6 %copy-done.1 = bf16[32,256,128]{2,1,0:T(8,128)(2,1)S(1)} copy-done((bf16[32,256,128]{2,1,0:T(8,128)(2,1)S(1)}, bf16[32,256,128]{2,1,0:T(8,128)(2,1)}, u32[]{:S(2)}) %copy-start.1) | copy-done | bytes 2097176
  6.9 0.0 copy-start.2
  6.9 0.9 copy-done.2
  7.8 0.0 copy-start.4
  7.8 0.7 copy-done.4
  8.5 108.0 %row_attention.1 = (bf16[8,32,64,128]{3,2,1,0:T(8,128)(2,1)}, f32[32,1024]{1,0:T(8,128)S(1)}) custom-call(bf16[2,64,64,256]{3,2,1,0:T(8,128)(2,1)} %bitcast.25, s32[2,64,256]{2,1,0:T(8,128)S(1)} %bitcast.18, f32[256,128]{1,0:T(8,128)S(1)} %convert_bitcast_fusion.mt_ref, bf16[32,256,128]{2,1,0:T(8,128)(2,1)S(1)} %copy-done.1, bf16[8,128]{1,0:T(8,128)(2,1)S(1)} %bitcast.24, ...), custom_call_target="tpu_custom_call" | custom-call | tf_op jit(solution)/shard_map/row_attention/pallas_call | solution.py:274
  116.6 0.0 copy-done.3
  116.6 0.0 copy-start
  116.6 2.2 %copy-done = bf16[8,32,64,128]{3,2,1,0:T(8,128)(2,1)S(1)} copy-done((bf16[8,32,64,128]{3,2,1,0:T(8,128)(2,1)S(1)}, bf16[8,32,64,128]{3,2,1,0:T(8,128)(2,1)}, u32[]{:S(2)}) %copy-start) | copy-done | bytes 4194328
  118.8 38.6 %column_and_transition.1 = bf16[32,64,1024]{2,1,0:T(8,128)(2,1)} custom-call(bf16[8,32,64,128]{3,2,1,0:T(8,128)(2,1)S(1)} %copy-done, f32[32,1024]{1,0:T(8,128)S(1)} %get-tuple-element.8.m_ref, bf16[256,64]{1,0:T(8,128)(2,1)S(1)} %pad_maximum_fusion.wc_ref, bf16[64,64]{1,0:T(8,128)(2,1)S(1)} %bitcast.21, bf16[256,64]{1,0:T(8,128)(2,1)S(1)} %bitcast.19, ...), custom_call_target="tpu_custom_call" | custom-call | tf_op jit(solution)/shard_map/column_and_transition/pallas_call | solution.py:366
  (5 shorter events, 0.0 us)
Async XLA Ops:
  0.0 116.6 %copy-start.3 = (bf16[256,64]{0,1:T(8,128)(2,1)S(1)}, bf16[256,64]{0,1:T(8,128)(2,1)}, u32[]{:S(2)}) copy-start(bf16[256,64]{0,1:T(8,128)(2,1)} %param.19) | copy-start | bytes 98308
  5.3 1.6 %copy-start.1 = (bf16[32,256,128]{2,1,0:T(8,128)(2,1)S(1)}, bf16[32,256,128]{2,1,0:T(8,128)(2,1)}, u32[]{:S(2)}) copy-start(bf16[32,256,128]{2,1,0:T(8,128)(2,1)} %z_ref.1) | copy-start | bytes 6291460
  6.9 0.9 copy-start.2
  7.8 0.7 copy-start.4
  116.6 2.2 %copy-start = (bf16[8,32,64,128]{3,2,1,0:T(8,128)(2,1)S(1)}, bf16[8,32,64,128]{3,2,1,0:T(8,128)(2,1)}, u32[]{:S(2)}) copy-start(bf16[8,32,64,128]{3,2,1,0:T(8,128)(2,1)} %get-tuple-element.7.r_ref) | copy-start | bytes 12582916

commit v3 on v2

v3 whole, which is shorter than its diff:
```python
import functools

import jax
import jax.numpy as jnp
import numpy as np
from jax import lax
from jax.experimental import pallas as pl
from jax.experimental.pallas import tpu as pltpu
from jax.sharding import PartitionSpec as P

LN_EPS = 1.0e-5
MASK_BIG = 1.0e9
MEAN_EPS = 1.0e-10
LOG2E = 1.4426950408889634
BF = jnp.bfloat16
F32 = jnp.float32
MESH = pl.DeviceIdType.MESH

VMEM_BYTES = 67_043_328

TILE_PAIRS = 8
ROW_TIME = dict(norm=-6, project=-5, split=-3, logits=0, softmax=4, values=5, divide=8, gate=9, out=10, emit=11)
ROW_ORDER = ('logits', 'values', 'project', 'out', 'softmax', 'norm', 'split', 'divide', 'gate', 'emit')
TILE_RES = 16
COL_STAGES = (('finish', 5), ('hidden', 4), ('out', 3), ('logits', 2), ('project', 1), ('turn', 0), ('softmax', 2), ('q_mean', 1))
BIAS_ROWS = 16


def norm_rows(x):
    n = x.shape[0]
    mean = jnp.sum(x, axis=0, keepdims=True) * (1.0 / n)
    centered = x - mean
    var = jnp.sum(centered * centered, axis=0, keepdims=True) * (1.0 / n)
    return (centered * lax.rsqrt(var + LN_EPS)).astype(BF)


def dot(a, b):
    return lax.dot_general(a, b, (((1,), (0,)), ((), ())), preferred_element_type=F32)


def dot_nt(a, b):
    return lax.dot_general(a, b, (((1,), (1,)), ((), ())), preferred_element_type=F32)


def split_bf16(value, parts):
    out, rest = [], np.float64(value)
    for _ in range(parts):
        part = np.float64(np.asarray(rest, np.float32).astype(np.dtype(BF)))
        out.append(float(part))
        rest = rest - part
    return out


def transposed(w):
    return w.astype(F32).T.astype(BF)


def row_stream(loads, w_in_t, w_out_t, bias_ref, n_heads, n_res, emit):
    width = w_out_t.shape[1]
    d = width // n_heads
    row_id = lax.broadcasted_iota(jnp.int32, (16, n_res), 0)
    mask_rows = jnp.zeros((16, n_res), F32)
    for n, term in enumerate(split_bf16(MASK_BIG * LOG2E, 3)):
        mask_rows = jnp.where(row_id == n, term, mask_rows)
    mask_rows = mask_rows.astype(BF)
    per_tile = 16 // d
    zero = jnp.zeros((16, n_res), BF)
    ones = jnp.ones((8, n_res), F32)
    state = [dict() for _ in loads]

    def norm(i, h):
        x_bf, m_row = loads[i]()
        x = x_bf.astype(F32)
        state[i].update(x=x, m_row=m_row, y=norm_rows(x))

    def project(i, h):
        state[i]['proj'] = dot(w_in_t, state[i].pop('y')).astype(BF)

    def split(i, h):
        s = state[i]
        proj = s.pop('proj')
        q = proj[:width].astype(F32) * (d ** -0.5 * LOG2E)
        q_hi = q.astype(BF)
        k = proj[width:2 * width]
        m_rows = jnp.broadcast_to(s.pop('m_row') - 1.0, (16, n_res)).astype(BF)
        s.update(q_hi=q_hi, q_lo=(q - q_hi.astype(F32)).astype(BF), v=proj[2 * width:3 * width], g=proj[3 * width:],
                 keys=jnp.concatenate([k, k, m_rows], axis=0).T)

    def only_head(q, h):
        mine = h // per_tile
        own = jnp.where(row_id // d == h % per_tile, q[mine * 16:(mine + 1) * 16], zero)
        return [own if n == mine else zero for n in range(width // 16)]

    def logits(i, h):
        s = state[i]
        rhs = jnp.concatenate(only_head(s['q_hi'], h) + only_head(s['q_lo'], h) + [mask_rows], axis=0)
        s['t', h] = dot(s['keys'], rhs) + bias_ref[h]

    def softmax(i, h):
        t = state[i].pop(('t', h))
        state[i]['p', h] = jnp.exp2(t - jnp.max(t, axis=0, keepdims=True)).astype(BF)

    def values(i, h):
        s = state[i]
        lhs = jnp.concatenate([s['v'][h * d:(h + 1) * d].astype(F32), ones], axis=0).astype(BF)
        s['o', h] = dot(lhs, s.pop(('p', h)))

    def divide(i, h):
        o = state[i].pop(('o', h))
        state[i]['r', h] = o[:d] / o[d:d + 8]

    def gate(i, h):
        s = state[i]
        o = jnp.concatenate([s.pop(('r', n)) for n in range(n_heads)], axis=0)
        s['gated'] = (jax.nn.sigmoid(s.pop('g').astype(F32)) * o).astype(BF)

    def out(i, h):
        state[i]['u'] = dot(w_out_t, state[i].pop('gated'))

    def last(i, h):
        s = state[i]
        emit(i, (s.pop('x') + s.pop('u')).astype(BF))
        s.clear()

    stages = dict(norm=norm, project=project, split=split, logits=logits, softmax=softmax, values=values, divide=divide,
                  gate=gate, out=out, emit=last)
    first, end = ('norm', 'project', 'split'), ('gate', 'out', 'emit')
    events = []
    for i in range(len(loads)):
        for rank, name in enumerate(ROW_ORDER):
            heads = [0] if name in first else [n_heads - 1] if name in end else range(n_heads)
            events += [(n_heads * i + h + ROW_TIME[name], rank, i, h, name) for h in heads]
    for _, _, i, h, name in sorted(events):
        stages[name](i, h)


def row_kernel(n_dev, e_ref, m_ref, z_hbm, w_pair_ref, w_in_ref, w_out_ref, recv_ref, mrecv_ref,
               turned, outbox, z_ref, mt_ref, bias_rows, bias_all, bias_ref, send_sem, recv_sem, own_sem, msend_sem, mrecv_sem,
               mown_sem, z_sem, bsend_sem, brecv_sem, fsend_sem, frecv_sem):
    t = pl.program_id(0)
    n_tiles = pl.num_programs(0)
    static_tiles = recv_sem.shape[0]
    me = lax.axis_index('seq')
    n_heads, _, n_res = bias_ref.shape
    pairs = e_ref.shape[1]
    share = n_res // n_dev
    n_local = mt_ref.shape[1]
    chans = turned.shape[1]

    def peer(k):
        return lax.rem(me + k, n_dev)

    def mask_copy(k):
        d = peer(k)
        return pltpu.make_async_remote_copy(
            src_ref=mt_ref.at[pl.ds(pl.multiple_of(d * share, share), share)],
            dst_ref=mrecv_ref.at[:, pl.ds(pl.multiple_of(me * n_local, n_local), n_local)],
            send_sem=msend_sem.at[k], recv_sem=mrecv_sem.at[k], device_id={'seq': d}, device_id_type=MESH)

    def mask_own():
        return pltpu.make_async_copy(
            mt_ref.at[pl.ds(pl.multiple_of(me * share, share), share)],
            mrecv_ref.at[:, pl.ds(pl.multiple_of(me * n_local, n_local), n_local)], mown_sem)

    def tile_copy(tile, k):
        d = peer(k)
        slot = lax.rem(tile, 2)
        return pltpu.make_async_remote_copy(
            src_ref=outbox.at[slot, pl.ds(d * share, share)],
            dst_ref=recv_ref.at[me, :, pl.ds(pl.multiple_of(tile * pairs, pairs), pairs), :],
            send_sem=send_sem.at[slot, k], recv_sem=recv_sem.at[tile, k], device_id={'seq': d}, device_id_type=MESH)

    def tile_own(tile):
        slot = lax.rem(tile, 2)
        return pltpu.make_async_copy(
            outbox.at[slot, pl.ds(me * share, share)],
            recv_ref.at[me, :, pl.ds(pl.multiple_of(tile * pairs, pairs), pairs), :], own_sem.at[slot])

    chunks = share // BIAS_ROWS
    others = n_dev // 2
    partner = me + 1 - 2 * lax.rem(me, 2)

    def bias_block(owner, c):
        return bias_all.at[:, pl.ds(pl.multiple_of(owner * share + c * BIAS_ROWS, BIAS_ROWS), BIAS_ROWS), :]

    def bias_copy(c, q):
        to = partner if q == 0 else lax.rem(me + 2 * q, n_dev)
        return pltpu.make_async_remote_copy(
            src_ref=bias_block(me, c), dst_ref=bias_block(me, c), send_sem=bsend_sem.at[c, q], recv_sem=brecv_sem.at[c, q],
            device_id={'seq': to}, device_id_type=MESH)

    def bias_forward(c, q):
        owner = lax.rem(me + n_dev - 2 * q, n_dev)
        return pltpu.make_async_remote_copy(
            src_ref=bias_block(owner, c), dst_ref=bias_block(owner, c), send_sem=fsend_sem.at[c, q],
            recv_sem=frecv_sem.at[c, q], device_id={'seq': partner}, device_id_type=MESH)

    def z_copy(c):
        rows = pl.ds(c * BIAS_ROWS, BIAS_ROWS)
        return pltpu.make_async_copy(z_hbm.at[rows], z_ref.at[rows], z_sem.at[c])

    @pl.when(t == 0)
    def _():
        for c in range(chunks):
            z_copy(c).start()
        barrier = pltpu.get_barrier_semaphore()
        for k in range(1, n_dev):
            pl.semaphore_signal(barrier, inc=1, device_id={'seq': peer(k)}, device_id_type=MESH)
        z_ch = z_ref.shape[2]
        eye = jnp.where(lax.broadcasted_iota(jnp.int32, (z_ch, z_ch), 0) == lax.broadcasted_iota(jnp.int32, (z_ch, z_ch), 1),
                        1.0, 0.0).astype(BF)
        w_pair = w_pair_ref[...]
        for c in range(chunks):
            z_copy(c).wait()

            def rows_step(n, carry, c=c):
                i = c * BIAS_ROWS + n * 4
                turned_z = dot_nt(eye, z_ref[pl.ds(i, 4)].reshape(4 * n_res, z_ch))
                b = dot(w_pair, norm_rows(turned_z))
                for u in range(4):
                    for part in range(n_res // 128):
                        at = u * n_res + part * 128
                        bias_rows[part, pl.ds(i + u, n_heads, stride=share), :] = b[:, at:at + 128]
                return carry

            lax.fori_loop(0, BIAS_ROWS // 4, rows_step, 0)
            for part in range(n_res // 128):
                own = bias_rows[part].reshape(n_heads, share, 128)[:, c * BIAS_ROWS:(c + 1) * BIAS_ROWS]
                bias_all[:, pl.ds(pl.multiple_of(me * share + c * BIAS_ROWS, BIAS_ROWS), BIAS_ROWS),
                         part * 128:(part + 1) * 128] = own.astype(BF)
            if c == 0:
                pl.semaphore_wait(barrier, n_dev - 1)
            for q in range(others):
                bias_copy(c, q).start()
        mt_ref[...] = m_ref[...].reshape(2 * m_ref.shape[1], n_res).astype(F32).T
        for c in range(chunks):
            for q in range(1, others):
                bias_copy(c, q).wait_recv()
                bias_forward(c, q).start()
        for k in range(1, n_dev):
            mask_copy(k).start()
        mask_own().start()
        for c in range(chunks):
            bias_copy(c, 0).wait_recv()
            for q in range(1, others):
                bias_forward(c, q).wait_recv()

        def turn(h, carry):
            bias_ref[h] = bias_all[h].astype(F32).T * LOG2E
            return carry

        lax.fori_loop(0, n_heads, turn, 0)
        for c in range(chunks):
            for q in range(others):
                bias_copy(c, q).wait_send()
            for q in range(1, others):
                bias_forward(c, q).wait_send()

    def load(u):
        row = pl.ds(t * pairs + u // 2, 1)
        return lambda: (e_ref[u % 2, u // 2], m_ref[u % 2, row, :].astype(F32))

    done = {}

    def emit(u, e1):
        done[u] = e1.astype(F32)
        if u % 2:
            turned[pl.ds(u // 2, n_res, stride=pairs), :] = jnp.concatenate([done.pop(u - 1), done.pop(u)], axis=0).T

    row_stream([load(u) for u in range(2 * pairs)], transposed(w_in_ref[...]), transposed(w_out_ref[...]), bias_ref, n_heads,
               n_res, emit)

    @pl.when(t >= 2)
    def _():
        for k in range(1, n_dev):
            tile_copy(t - 2, k).wait_send()
        tile_own(t - 2).wait()

    outbox[lax.rem(t, 2)] = turned[...].reshape(n_res, pairs, chans).astype(BF)
    for k in range(1, n_dev):
        tile_copy(t, k).start()
    tile_own(t).start()

    @pl.when(t == n_tiles - 1)
    def _():
        for tile in range(max(static_tiles - 2, 0), static_tiles):
            for k in range(1, n_dev):
                tile_copy(tile, k).wait_send()
            tile_own(tile).wait()
        for k in range(1, n_dev):
            mask_copy(k).wait_send()
            mask_copy(k).wait_recv()
        mask_own().wait()
        for tile in range(static_tiles):
            for k in range(1, n_dev):
                tile_copy(tile, k).wait_recv()


def row_attention(n_dev, e_t, mask, pair, w_pair_t, w_in, w_out):
    n_seq, chans, n_res = e_t.shape
    half = n_seq // 2
    tiles = half // TILE_PAIRS
    share = n_res // n_dev
    n_heads = w_pair_t.shape[0]
    e_t = e_t.reshape(2, half, chans, n_res)
    mask = mask.reshape(2, half, n_res)

    def whole(a):
        return pl.BlockSpec(a.shape, lambda t: (0,) * a.ndim)

    return pl.pallas_call(
        functools.partial(row_kernel, n_dev),
        grid=(tiles,),
        in_specs=[
            pl.BlockSpec((2, TILE_PAIRS, chans, n_res), lambda t: (0, t, 0, 0)),
            whole(mask), pl.BlockSpec(memory_space=pl.ANY), whole(w_pair_t), whole(w_in), whole(w_out),
        ],
        out_specs=[pl.BlockSpec(memory_space=pl.ANY), pl.BlockSpec(memory_space=pl.ANY)],
        out_shape=[
            jax.ShapeDtypeStruct((n_dev, share, half, 2 * chans), BF),
            jax.ShapeDtypeStruct((share, n_dev * n_seq), F32),
        ],
        scratch_shapes=[
            pltpu.VMEM((n_res * TILE_PAIRS, 2 * chans), F32),
            pltpu.VMEM((2, n_res, TILE_PAIRS, 2 * chans), BF),
            pltpu.VMEM(pair.shape, BF),
            pltpu.VMEM((n_res, n_seq), F32),
            pltpu.VMEM((n_res // 128, n_heads * share, 128), F32),
            pltpu.VMEM((n_heads, n_res, n_res), BF),
            pltpu.VMEM((n_heads, n_res, n_res), F32),
            pltpu.SemaphoreType.DMA((2, n_dev)),
            pltpu.SemaphoreType.DMA((tiles, n_dev)),
            pltpu.SemaphoreType.DMA((2,)),
            pltpu.SemaphoreType.DMA((n_dev,)),
            pltpu.SemaphoreType.DMA((n_dev,)),
            pltpu.SemaphoreType.DMA,
            pltpu.SemaphoreType.DMA((share // BIAS_ROWS,)),
        ] + [pltpu.SemaphoreType.DMA((share // BIAS_ROWS, n_dev // 2))] * 4,
        compiler_params=pltpu.CompilerParams(
            dimension_semantics=('arbitrary',), vmem_limit_bytes=VMEM_BYTES, collective_id=0, has_side_effects=True),
        name='row_attention',
    )(e_t, mask, pair, w_pair_t, w_in, w_out)


def col_kernel(n_heads, r_ref, m_ref, wc_ref, wco_ref, wti_ref, wto_ref, o_ref):
    n_dev, n_i, half, lanes = r_ref.shape
    chans = lanes // 2
    width = wco_ref.shape[0]
    d = width // n_heads
    eye = jnp.where(lax.broadcasted_iota(jnp.int32, (lanes, lanes), 0) == lax.broadcasted_iota(jnp.int32, (lanes, lanes), 1),
                    1.0, 0.0).astype(BF)
    low = lax.broadcasted_iota(jnp.int32, (chans, 2 * half), 1) < half
    same_head = (lax.broadcasted_iota(jnp.int32, (width, width), 0) // d
                 == lax.broadcasted_iota(jnp.int32, (width, width), 1) // d)
    w_t = wc_ref[...].astype(F32).T
    wc = jnp.concatenate([w_t[:width]] + [w_t[width:width + d]] * n_heads + [w_t[width + d:width + 2 * d]] * n_heads
                         + [w_t[width + 2 * d:]], axis=0).astype(BF)
    wco, wti, wto = transposed(wco_ref[...]), transposed(wti_ref[...]), wto_ref[...]
    state = [dict() for _ in range(n_i)]

    def turn(i):
        state[i]['turned'] = dot_nt(eye, r_ref[:, i].reshape(n_dev * half, lanes))

    def project(i):
        s = state[i]
        turned = s.pop('turned')
        cols = []
        for n in range(n_dev // 2):
            a = turned[:chans, n * 2 * half:(n + 1) * 2 * half]
            b = turned[chans:, n * 2 * half:(n + 1) * 2 * half]
            cols.append(jnp.where(low, a, pltpu.roll(b, half, 1)))
            cols.append(jnp.where(low, pltpu.roll(a, half, 1), b))
        s['x'] = jnp.concatenate(cols, axis=1)
        s['proj'] = dot(wc, norm_rows(s['x'])).astype(BF)

    def q_mean(i):
        s = state[i]
        m = m_ref[pl.ds(i, 1), :]
        q_sum = jnp.sum(s['proj'][:width].astype(F32) * m, axis=1, keepdims=True)
        count = jnp.sum(m, axis=1, keepdims=True)
        mean = jnp.broadcast_to(q_sum / (count + MEAN_EPS), (width, width))
        s['q_rows'] = jnp.where(same_head, mean.T, 0.0).astype(BF)

    def logits(i):
        s = state[i]
        s['logits'] = dot(s.pop('q_rows'), s['proj'][width:2 * width])

    def softmax(i):
        s = state[i]
        proj = s.pop('proj')
        t = s.pop('logits') * (d ** -0.5) + MASK_BIG * (m_ref[pl.ds(i, 1), :] - 1.0)
        e = jnp.exp(t - jnp.max(t, axis=1, keepdims=True))
        den = jnp.sum(e, axis=1, keepdims=True)
        num = jnp.sum(e * proj[2 * width:3 * width].astype(F32), axis=1, keepdims=True)
        s['gated'] = (jax.nn.sigmoid(proj[3 * width:].astype(F32)) * (num / den)).astype(BF)

    def out(i):
        s = state[i]
        s['e2'] = (s.pop('x') + dot(wco, s.pop('gated'))).astype(BF)

    def hidden(i):
        s = state[i]
        s['hidden'] = jnp.maximum(dot(wti, norm_rows(s['e2'].astype(F32))), 0.0).astype(BF)

    def finish(i):
        s = state[i]
        o_ref[i] = (s.pop('e2').astype(F32) + dot(wto, s.pop('hidden'))).astype(BF)

    stages = dict(turn=turn, project=project, q_mean=q_mean, logits=logits, softmax=softmax, out=out, hidden=hidden, finish=finish)
    for step in range(n_i + max(lag for _, lag in COL_STAGES)):
        for name, lag in COL_STAGES:
            if 0 <= step - lag < n_i:
                stages[name](step - lag)


def column_and_transition(n_heads, received, mask, wc, wco, wti, wto):
    n_dev, share, half, lanes = received.shape
    n_seq = mask.shape[1]

    def whole(a):
        return pl.BlockSpec(a.shape, lambda n: (0,) * a.ndim)

    return pl.pallas_call(
        functools.partial(col_kernel, n_heads),
        grid=(share // TILE_RES,),
        in_specs=[
            pl.BlockSpec((n_dev, TILE_RES, half, lanes), lambda n: (0, n, 0, 0)),
            pl.BlockSpec((TILE_RES, n_seq), lambda n: (n, 0)),
            whole(wc), whole(wco), whole(wti), whole(wto),
        ],
        out_specs=pl.BlockSpec((TILE_RES, lanes // 2, n_seq), lambda n: (n, 0, 0)),
        out_shape=jax.ShapeDtypeStruct((share, lanes // 2, n_seq), BF),
        compiler_params=pltpu.CompilerParams(dimension_semantics=('arbitrary',), vmem_limit_bytes=VMEM_BYTES),
        name='column_and_transition',
    )(received, mask, wc, wco, wti, wto)


def solution(mesh):
    n_dev = mesh.shape['seq']

    def local_block(msa, mask, pair, w_pair_bias, w_row_in, w_row_out, w_col_in, w_col_out, w_trans_in, w_trans_out):
        n_heads = w_pair_bias.shape[1]
        received, mask_cols = row_attention(
            n_dev, jnp.transpose(msa, (0, 2, 1)), mask, pair, w_pair_bias.T, w_row_in, w_row_out)
        out = column_and_transition(n_heads, received, mask_cols, w_col_in, w_col_out, w_trans_in, w_trans_out.T)
        return jnp.transpose(out, (2, 0, 1))

    rows = P(('batch', 'seq'))
    return jax.shard_map(local_block, mesh=mesh, in_specs=(rows, rows, rows) + (P(),) * 7, out_specs=P('batch', 'seq'),
                         check_vma=False)
```

time: 158 us -> 121 us (0.77)
  Pallas kernels: 147 us -> 121 us
  local copies, waits for them, and re-layouts: 10.6 us -> 0 us
    pallas_call x1, Pallas kernels: 38.6 us -> 22.3 us  [column_and_transition(): pl.pallas_call(functools.partial(col_kernel, n_heads), grid=(share // TIL...]
    unnamed x16 -> x0, local copies, waits for them, and re-layouts: 10.6 us -> none
    pallas_call x1, Pallas kernels: 108 us -> 98.7 us  [row_attention(): pl.pallas_call(functools.partial(row_kernel, n_dev), grid=(tiles,), in_sp...]
where the time goes in v3:
time: 121 us
  Pallas kernels  121 us (100%)
    pallas_call x1, Pallas kernels, row_attention(): pl.pallas_call(functools.partial(row_kernel, n_dev), grid=(tiles,), in_sp...  98.7 us
    pallas_call x1, Pallas kernels, column_and_transition(): pl.pallas_call(functools.partial(col_kernel, n_heads), grid=(share // TIL...  22.3 us

profile of v3, /device:TPU:81, one launch (start us, length us, event | category | flops | bytes accessed | tf_op | source)
XLA Modules:
  0.0 121.0 jit_solution(6493607570145451391)
XLA Ops:
  0.0 98.7 %row_attention.1 = (bf16[8,32,64,128]{3,2,1,0:T(8,128)(2,1)}, f32[32,1024]{1,0:T(8,128)}) custom-call(bf16[2,64,64,256]{3,2,1,0:T(8,128)(2,1)} %bitcast.7, s32[2,64,256]{2,1,0:T(8,128)} %bitcast.8, bf16[32,256,128]{2,1,0:T(8,128)(2,1)} %z_hbm.1, bf16[8,128]{1,0:T(8,128)(2,1)} %bitcast.10, bf16[64,256]{1,0:T(8,128)(2,1)} %w_in_ref.1, bf16[64,64]{1,0:T(8,128)(2,1)} %w_out_ref.1), custom_call_target="tpu_custom_call" | custom-call | tf_op jit(solution)/shard_map/row_attention/pallas_call | solution.py:311
  98.7 22.3 %column_and_transition.1 = bf16[32,64,1024]{2,1,0:T(8,128)(2,1)} custom-call(bf16[8,32,64,128]{3,2,1,0:T(8,128)(2,1)} %get-tuple-element.7.r_ref, f32[32,1024]{1,0:T(8,128)} %get-tuple-element.8.m_ref, bf16[64,144]{1,0:T(8,128)(2,1)} %wc_ref.1, bf16[64,64]{1,0:T(8,128)(2,1)} %wco_ref.1, bf16[64,256]{1,0:T(8,128)(2,1)} %wti_ref.1, bf16[64,256]{1,0:T(8,128)(2,1)} %bitcast.9), custom_call_target="tpu_custom_call" | custom-call | tf_op jit(solution)/shard_map/column_and_transition/pallas_call | solution.py:423

commit v4 on v3

--- a/solution.py
+++ b/solution.py
@@ -24,6 +24,7 @@
 TILE_RES = 16
 COL_STAGES = (('finish', 5), ('hidden', 4), ('out', 3), ('logits', 2), ('project', 1), ('turn', 0), ('softmax', 2), ('q_mean', 1))
 BIAS_ROWS = 16
+FAR = 6
 
 
 def norm_rows(x):
@@ -55,7 +56,37 @@
     return w.astype(F32).T.astype(BF)
 
 
-def row_stream(loads, w_in_t, w_out_t, bias_ref, n_heads, n_res, emit):
+class Prologue:
+    def __init__(self, w_in_t, width, head_dim):
+        self.w_in_t, self.width, self.head_dim = w_in_t, width, head_dim
+
+    def norm(self, s, x_bf, m_row):
+        x = x_bf.astype(F32)
+        s.update(x=x, m_row=m_row, y=norm_rows(x))
+
+    def project(self, s):
+        s['proj'] = dot(self.w_in_t, s.pop('y')).astype(BF)
+
+    def split(self, s):
+        width = self.width
+        proj = s.pop('proj')
+        q = proj[:width].astype(F32) * (self.head_dim ** -0.5 * LOG2E)
+        q_hi = q.astype(BF)
+        k = proj[width:2 * width]
+        m_rows = jnp.broadcast_to(s.pop('m_row') - 1.0, (16, proj.shape[1])).astype(BF)
+        s.update(q_hi=q_hi, q_lo=(q - q_hi.astype(F32)).astype(BF), v=proj[2 * width:3 * width], g=proj[3 * width:],
+                 keys=jnp.concatenate([k, k, m_rows], axis=0).T)
+
+    def save(self, s, kept_ref, keys_ref):
+        kept_ref[...] = jnp.concatenate([s['q_hi'], s['q_lo'], s['v'], s['g']], axis=0)
+        keys_ref[...] = s['keys']
+
+    def restore(self, x_bf, kept_ref, keys_ref):
+        q_hi, q_lo, v, g = (kept_ref[n * self.width:(n + 1) * self.width] for n in range(4))
+        return dict(x=x_bf.astype(F32), q_hi=q_hi, q_lo=q_lo, v=v, g=g, keys=keys_ref[...])
+
+
+def row_stream(loads, first, prologue, save_next, w_out_t, bias_ref, n_heads, n_res, emit):
     width = w_out_t.shape[1]
     d = width // n_heads
     row_id = lax.broadcasted_iota(jnp.int32, (16, n_res), 0)
@@ -66,25 +97,18 @@
     per_tile = 16 // d
     zero = jnp.zeros((16, n_res), BF)
     ones = jnp.ones((8, n_res), F32)
-    state = [dict() for _ in loads]
+    state = [first] + [dict() for _ in loads[1:]]
 
     def norm(i, h):
-        x_bf, m_row = loads[i]()
-        x = x_bf.astype(F32)
-        state[i].update(x=x, m_row=m_row, y=norm_rows(x))
+        prologue.norm(state[i], *loads[i]())
 
     def project(i, h):
-        state[i]['proj'] = dot(w_in_t, state[i].pop('y')).astype(BF)
+        prologue.project(state[i])
 
     def split(i, h):
-        s = state[i]
-        proj = s.pop('proj')
-        q = proj[:width].astype(F32) * (d ** -0.5 * LOG2E)
-        q_hi = q.astype(BF)
-        k = proj[width:2 * width]
-        m_rows = jnp.broadcast_to(s.pop('m_row') - 1.0, (16, n_res)).astype(BF)
-        s.update(q_hi=q_hi, q_lo=(q - q_hi.astype(F32)).astype(BF), v=proj[2 * width:3 * width], g=proj[3 * width:],
-                 keys=jnp.concatenate([k, k, m_rows], axis=0).T)
+        prologue.split(state[i])
+        if i == len(loads) - 1:
+            save_next(state[i])
 
     def only_head(q, h):
         mine = h // per_tile
@@ -124,18 +148,20 @@
 
     stages = dict(norm=norm, project=project, split=split, logits=logits, softmax=softmax, values=values, divide=divide,
                   gate=gate, out=out, emit=last)
-    first, end = ('norm', 'project', 'split'), ('gate', 'out', 'emit')
+    first_stages, end = ('norm', 'project', 'split'), ('gate', 'out', 'emit')
     events = []
     for i in range(len(loads)):
         for rank, name in enumerate(ROW_ORDER):
-            heads = [0] if name in first else [n_heads - 1] if name in end else range(n_heads)
+            if (i == 0 and name in first_stages) or (i == len(loads) - 1 and name not in first_stages):
+                continue
+            heads = [0] if name in first_stages else [n_heads - 1] if name in end else range(n_heads)
             events += [(n_heads * i + h + ROW_TIME[name], rank, i, h, name) for h in heads]
     for _, _, i, h, name in sorted(events):
         stages[name](i, h)
 
 
-def row_kernel(n_dev, e_ref, m_ref, z_hbm, w_pair_ref, w_in_ref, w_out_ref, recv_ref, mrecv_ref,
-               turned, outbox, z_ref, mt_ref, bias_rows, bias_all, bias_ref, send_sem, recv_sem, own_sem, msend_sem, mrecv_sem,
+def row_kernel(n_dev, e_ref, e_next_ref, m_ref, z_hbm, w_pair_ref, w_in_ref, w_out_ref, recv_ref, mrecv_ref,
+               turned, outbox, z_ref, mt_ref, bias_rows, bias_all, bias_ref, kept_ref, keys_ref, relay, relay_sem, on_sem, send_sem, recv_sem, own_sem, msend_sem, mrecv_sem,
                mown_sem, z_sem, bsend_sem, brecv_sem, fsend_sem, frecv_sem):
     t = pl.program_id(0)
     n_tiles = pl.num_programs(0)
@@ -147,8 +173,17 @@
     n_local = mt_ref.shape[1]
     chans = turned.shape[1]
 
+    def wrap(i):
+        return lax.rem(i + n_dev, n_dev)
+
+    def mate(i):
+        return i + 1 - 2 * lax.rem(i, 2)
+
+    ahead_chip, behind_chip, far_chip = wrap(me + 2), wrap(me - 2), wrap(me + n_dev // 2)
+    peers = [me, mate(me), ahead_chip, mate(ahead_chip), behind_chip, mate(behind_chip), far_chip, mate(far_chip)]
+
     def peer(k):
-        return lax.rem(me + k, n_dev)
+        return peers[k]
 
     def mask_copy(k):
         d = peer(k)
@@ -170,6 +205,33 @@
             dst_ref=recv_ref.at[me, :, pl.ds(pl.multiple_of(tile * pairs, pairs), pairs), :],
             send_sem=send_sem.at[slot, k], recv_sem=recv_sem.at[tile, k], device_id={'seq': d}, device_id_type=MESH)
 
+    def relay_out(tile, r):
+        slot = lax.rem(tile, 2)
+        return pltpu.make_async_remote_copy(
+            src_ref=outbox.at[slot, pl.ds(peer(FAR + r) * share, share)], dst_ref=relay.at[tile, r],
+            send_sem=send_sem.at[slot, FAR + r], recv_sem=relay_sem.at[tile, r],
+            device_id={'seq': (ahead_chip, behind_chip)[r]}, device_id_type=MESH)
+
+    def relay_on(tile, r):
+        owner = (behind_chip, ahead_chip)[r]
+        to = (ahead_chip, mate(behind_chip))[r]
+        return pltpu.make_async_remote_copy(
+            src_ref=relay.at[tile, r],
+            dst_ref=recv_ref.at[owner, :, pl.ds(pl.multiple_of(tile * pairs, pairs), pairs), :],
+            send_sem=on_sem.at[tile, r], recv_sem=recv_sem.at[tile, FAR + r], device_id={'seq': to}, device_id_type=MESH)
+
+    def wait_sent(tile):
+        for k in range(1, FAR):
+            tile_copy(tile, k).wait_send()
+        for r in range(2):
+            relay_out(tile, r).wait_send()
+        tile_own(tile).wait()
+
+    def pass_on(tile):
+        for r in range(2):
+            relay_out(tile, r).wait_recv()
+            relay_on(tile, r).start()
+
     def tile_own(tile):
         slot = lax.rem(tile, 2)
         return pltpu.make_async_copy(
@@ -198,6 +260,12 @@
     def z_copy(c):
         rows = pl.ds(c * BIAS_ROWS, BIAS_ROWS)
         return pltpu.make_async_copy(z_hbm.at[rows], z_ref.at[rows], z_sem.at[c])
+
+    width = w_out_ref.shape[0]
+    prologue = Prologue(transposed(w_in_ref[...]), width, width // n_heads)
+
+    def mask_row(half, row):
+        return m_ref[half, pl.ds(row, 1), :].astype(F32)
 
     @pl.when(t == 0)
     def _():
@@ -213,17 +281,15 @@
         for c in range(chunks):
             z_copy(c).wait()
 
-            def rows_step(n, carry, c=c):
-                i = c * BIAS_ROWS + n * 4
-                turned_z = dot_nt(eye, z_ref[pl.ds(i, 4)].reshape(4 * n_res, z_ch))
-                b = dot(w_pair, norm_rows(turned_z))
+            at = [c * BIAS_ROWS + n for n in range(0, BIAS_ROWS, 4)]
+            turned_z = [dot_nt(eye, z_ref[i:i + 4].reshape(4 * n_res, z_ch)) for i in at]
+            normed = [norm_rows(z) for z in turned_z]
+            b = [dot(w_pair, z) for z in normed]
+            for n, i in enumerate(at):
                 for u in range(4):
                     for part in range(n_res // 128):
-                        at = u * n_res + part * 128
-                        bias_rows[part, pl.ds(i + u, n_heads, stride=share), :] = b[:, at:at + 128]
-                return carry
-
-            lax.fori_loop(0, BIAS_ROWS // 4, rows_step, 0)
+                        lane = u * n_res + part * 128
+                        bias_rows[part, pl.ds(i + u, n_heads, stride=share), :] = b[n][:, lane:lane + 128]
             for part in range(n_res // 128):
                 own = bias_rows[part].reshape(n_heads, share, 128)[:, c * BIAS_ROWS:(c + 1) * BIAS_ROWS]
                 bias_all[:, pl.ds(pl.multiple_of(me * share + c * BIAS_ROWS, BIAS_ROWS), BIAS_ROWS),
@@ -232,6 +298,11 @@
                 pl.semaphore_wait(barrier, n_dev - 1)
             for q in range(others):
                 bias_copy(c, q).start()
+        ahead = {}
+        prologue.norm(ahead, e_ref[0, 0], mask_row(0, 0))
+        prologue.project(ahead)
+        prologue.split(ahead)
+        prologue.save(ahead, kept_ref, keys_ref)
         mt_ref[...] = m_ref[...].reshape(2 * m_ref.shape[1], n_res).astype(F32).T
         for c in range(chunks):
             for q in range(1, others):
@@ -245,11 +316,8 @@
             for q in range(1, others):
                 bias_forward(c, q).wait_recv()
 
-        def turn(h, carry):
+        for h in range(n_heads):
             bias_ref[h] = bias_all[h].astype(F32).T * LOG2E
-            return carry
-
-        lax.fori_loop(0, n_heads, turn, 0)
         for c in range(chunks):
             for q in range(others):
                 bias_copy(c, q).wait_send()
@@ -257,8 +325,10 @@
                 bias_forward(c, q).wait_send()
 
     def load(u):
-        row = pl.ds(t * pairs + u // 2, 1)
-        return lambda: (e_ref[u % 2, u // 2], m_ref[u % 2, row, :].astype(F32))
+        return lambda: (e_ref[u % 2, u // 2], mask_row(u % 2, t * pairs + u // 2))
+
+    def load_next():
+        return e_next_ref[0, 0], mask_row(0, lax.rem(t + 1, static_tiles) * pairs)
 
     done = {}
 
@@ -267,31 +337,36 @@
         if u % 2:
             turned[pl.ds(u // 2, n_res, stride=pairs), :] = jnp.concatenate([done.pop(u - 1), done.pop(u)], axis=0).T
 
-    row_stream([load(u) for u in range(2 * pairs)], transposed(w_in_ref[...]), transposed(w_out_ref[...]), bias_ref, n_heads,
-               n_res, emit)
+    row_stream([load(u) for u in range(2 * pairs)] + [load_next], prologue.restore(e_ref[0, 0], kept_ref, keys_ref), prologue,
+               lambda s: prologue.save(s, kept_ref, keys_ref), transposed(w_out_ref[...]), bias_ref, n_heads, n_res, emit)
 
     @pl.when(t >= 2)
     def _():
-        for k in range(1, n_dev):
-            tile_copy(t - 2, k).wait_send()
-        tile_own(t - 2).wait()
+        wait_sent(t - 2)
 
     outbox[lax.rem(t, 2)] = turned[...].reshape(n_res, pairs, chans).astype(BF)
-    for k in range(1, n_dev):
+    for r in range(2):
+        relay_out(t, r).start()
+    for k in (2, 4, 3, 5, 1):
         tile_copy(t, k).start()
     tile_own(t).start()
 
+    @pl.when(t >= 1)
+    def _():
+        pass_on(t - 1)
+
     @pl.when(t == n_tiles - 1)
     def _():
+        pass_on(static_tiles - 1)
         for tile in range(max(static_tiles - 2, 0), static_tiles):
-            for k in range(1, n_dev):
-                tile_copy(tile, k).wait_send()
-            tile_own(tile).wait()
+            wait_sent(tile)
         for k in range(1, n_dev):
             mask_copy(k).wait_send()
             mask_copy(k).wait_recv()
         mask_own().wait()
         for tile in range(static_tiles):
+            for r in range(2):
+                relay_on(tile, r).wait_send()
             for k in range(1, n_dev):
                 tile_copy(tile, k).wait_recv()
 
@@ -302,6 +377,7 @@
     tiles = half // TILE_PAIRS
     share = n_res // n_dev
     n_heads = w_pair_t.shape[0]
+    width = w_out.shape[0]
     e_t = e_t.reshape(2, half, chans, n_res)
     mask = mask.reshape(2, half, n_res)
 
@@ -313,6 +389,7 @@
         grid=(tiles,),
         in_specs=[
             pl.BlockSpec((2, TILE_PAIRS, chans, n_res), lambda t: (0, t, 0, 0)),
+            pl.BlockSpec((1, 1, chans, n_res), lambda t: (0, lax.rem(t + 1, tiles) * TILE_PAIRS, 0, 0)),
             whole(mask), pl.BlockSpec(memory_space=pl.ANY), whole(w_pair_t), whole(w_in), whole(w_out),
         ],
         out_specs=[pl.BlockSpec(memory_space=pl.ANY), pl.BlockSpec(memory_space=pl.ANY)],
@@ -328,6 +405,11 @@
             pltpu.VMEM((n_res // 128, n_heads * share, 128), F32),
             pltpu.VMEM((n_heads, n_res, n_res), BF),
             pltpu.VMEM((n_heads, n_res, n_res), F32),
+            pltpu.VMEM((4 * width, n_res), BF),
+            pltpu.VMEM((n_res, 2 * width + 16), BF),
+            pltpu.VMEM((tiles, 2, share, TILE_PAIRS, 2 * chans), BF),
+            pltpu.SemaphoreType.DMA((tiles, 2)),
+            pltpu.SemaphoreType.DMA((tiles, 2)),
             pltpu.SemaphoreType.DMA((2, n_dev)),
             pltpu.SemaphoreType.DMA((tiles, n_dev)),
             pltpu.SemaphoreType.DMA((2,)),
@@ -339,7 +421,7 @@
         compiler_params=pltpu.CompilerParams(
             dimension_semantics=('arbitrary',), vmem_limit_bytes=VMEM_BYTES, collective_id=0, has_side_effects=True),
         name='row_attention',
-    )(e_t, mask, pair, w_pair_t, w_in, w_out)
+    )(e_t, e_t, mask, pair, w_pair_t, w_in, w_out)
 
 
 def col_kernel(n_heads, r_ref, m_ref, wc_ref, wco_ref, wti_ref, wto_ref, o_ref):

time: 121 us -> 123 us (1.017)
    pallas_call x1, Pallas kernels: 98.7 us -> 100 us  [row_attention(): pl.pallas_call(functools.partial(row_kernel, n_dev), grid=(tiles,), in_sp...]
where the time goes in v4:
time: 123 us; the launch traced here: 122 us
  Pallas kernels  122 us (99%)
    pallas_call x1, Pallas kernels, row_attention(): pl.pallas_call(functools.partial(row_kernel, n_dev), grid=(tiles,), in_sp...  100 us
    pallas_call x1, Pallas kernels, column_and_transition(): pl.pallas_call(functools.partial(col_kernel, n_heads), grid=(share // TIL...  22.3 us

profile of v4, /device:TPU:81, one launch (start us, length us, event | category | flops | bytes accessed | tf_op | source)
XLA Modules:
  0.0 122.4 jit_solution(17846625043448298975)
XLA Ops:
  0.0 100.1 %row_attention.1 = (bf16[8,32,64,128]{3,2,1,0:T(8,128)(2,1)}, f32[32,1024]{1,0:T(8,128)}) custom-call(bf16[2,64,64,256]{3,2,1,0:T(8,128)(2,1)} %bitcast.7, bf16[2,64,64,256]{3,2,1,0:T(8,128)(2,1)} %bitcast.8, s32[2,64,256]{2,1,0:T(8,128)} %bitcast.9, bf16[32,256,128]{2,1,0:T(8,128)(2,1)} %z_hbm.1, bf16[8,128]{1,0:T(8,128)(2,1)} %bitcast.11, ...), custom_call_target="tpu_custom_call" | custom-call | tf_op jit(solution)/shard_map/row_attention/pallas_call | solution.py:387
  100.1 22.3 %column_and_transition.1 = bf16[32,64,1024]{2,1,0:T(8,128)(2,1)} custom-call(bf16[8,32,64,128]{3,2,1,0:T(8,128)(2,1)} %get-tuple-element.7.r_ref, f32[32,1024]{1,0:T(8,128)} %get-tuple-element.8.m_ref, bf16[64,144]{1,0:T(8,128)(2,1)} %wc_ref.1, bf16[64,64]{1,0:T(8,128)(2,1)} %wco_ref.1, bf16[64,256]{1,0:T(8,128)(2,1)} %wti_ref.1, bf16[64,256]{1,0:T(8,128)(2,1)} %bitcast.10), custom_call_target="tpu_custom_call" | custom-call | tf_op jit(solution)/shard_map/column_and_transition/pallas_call | solution.py:505

commit v5 on v3

--- a/solution.py
+++ b/solution.py
@@ -277,7 +277,7 @@
         tile_own(t - 2).wait()
 
     outbox[lax.rem(t, 2)] = turned[...].reshape(n_res, pairs, chans).astype(BF)
-    for k in range(1, n_dev):
+    for k in sorted(range(1, n_dev), key=lambda k: -min(k, n_dev - k)):
         tile_copy(t, k).start()
     tile_own(t).start()
 

time: 121 us -> 120 us (level)
  no operation moved by 1% of the time
where the time goes in v5:
time: 120 us
  Pallas kernels  120 us (100%)
    pallas_call x1, Pallas kernels, row_attention(): pl.pallas_call(functools.partial(row_kernel, n_dev), grid=(tiles,), in_sp...  97.6 us
    pallas_call x1, Pallas kernels, column_and_transition(): pl.pallas_call(functools.partial(col_kernel, n_heads), grid=(share // TIL...  22.3 us

profile of v5, /device:TPU:81, one launch (start us, length us, event | category | flops | bytes accessed | tf_op | source)
XLA Modules:
  0.0 119.9 jit_solution(6607720089993421447)
XLA Ops:
  0.0 97.6 %row_attention.1 = (bf16[8,32,64,128]{3,2,1,0:T(8,128)(2,1)}, f32[32,1024]{1,0:T(8,128)}) custom-call(bf16[2,64,64,256]{3,2,1,0:T(8,128)(2,1)} %bitcast.7, s32[2,64,256]{2,1,0:T(8,128)} %bitcast.8, bf16[32,256,128]{2,1,0:T(8,128)(2,1)} %z_hbm.1, bf16[8,128]{1,0:T(8,128)(2,1)} %bitcast.10, bf16[64,256]{1,0:T(8,128)(2,1)} %w_in_ref.1, bf16[64,64]{1,0:T(8,128)(2,1)} %w_out_ref.1), custom_call_target="tpu_custom_call" | custom-call | tf_op jit(solution)/shard_map/row_attention/pallas_call | solution.py:311
  97.6 22.3 %column_and_transition.1 = bf16[32,64,1024]{2,1,0:T(8,128)(2,1)} custom-call(bf16[8,32,64,128]{3,2,1,0:T(8,128)(2,1)} %get-tuple-element.7.r_ref, f32[32,1024]{1,0:T(8,128)} %get-tuple-element.8.m_ref, bf16[64,144]{1,0:T(8,128)(2,1)} %wc_ref.1, bf16[64,64]{1,0:T(8,128)(2,1)} %wco_ref.1, bf16[64,256]{1,0:T(8,128)(2,1)} %wti_ref.1, bf16[64,256]{1,0:T(8,128)(2,1)} %bitcast.9), custom_call_target="tpu_custom_call" | custom-call | tf_op jit(solution)/shard_map/column_and_transition/pallas_call | solution.py:423
